TPU v7x, 256 devices: a whole 4x4x8 slice. The times are simulated.
256 devices in a mesh: seq: 16 (over y_hi, x, core), exp: 16 (over y_lo, z).
Axes of the slice: x: 4, y: 4 (y_hi: 2, y_lo: 2; y = y_hi * 2 + y_lo), z: 8, core: 2. Of those that a mesh axis runs over, the one named last changes fastest.
Arguments:
- grad_out: bfloat16 [32768, 2048], P(('seq', 'exp')), may hold values from -6 to 6
- out_proj: bfloat16 [4096, 2048], P('exp'), may hold values from -0.125 to 0.125
- step_size: float32 [64, 32768], P('exp', 'seq'), may hold values from 0.001 to 0.1
- log_decay: float32 [64, 32768], P('exp', 'seq'), may hold values from -1 to 0, as said below
- b_input: float32 [16, 32768], P(None, 'seq'), may hold values from -1.5 to 1.5
- c_output: float32 [16, 32768], P(None, 'seq'), may hold values from -1.5 to 1.5
- skip_gain: float32 [4096], P('exp'), may hold values from 0.5 to 1.5
- expert_ids: int32 [32768, 2], P('seq'), may hold values from 0 to 15, all different within a row; in each aligned block of 128 rows (0 to 127, 128 to 255, ...) at most 18 rows name the same one
- hidden_act: bfloat16 [16, 256, 18, 8192], P('exp', None, None, 'seq'), may hold values from -6 to 6
- w_down: bfloat16 [16, 8192, 2048], P('exp', 'seq'), may hold values from -0.0029296875 to 0.0029296875
Outputs:
- d_inner: bfloat16 [32768, 4096], P('seq', 'exp')
- d_gate: float32 [2, 32768], P(None, ('seq', 'exp'))
Inputs may be any that keep to these rules, and one draw needn't show every extreme that they name: `expert_ids`: each row names 2 different experts. Within the rows of one token group no expert is named by more than 18 rows, and in every draw some expert is named by exactly 18 rows of some group. `log_decay`: every entry is negative.
All inputs are finite; a program needn't handle non-finite values.
Results may differ from a plain program's by a relative error of at most 0.00065.
Values may be sent and summed in bfloat16 or wider, within the bound.
A program may use at most 128 MiB of HBM per device.

v0:
```python
import jax
import jax.numpy as jnp
from jax import lax
from jax.sharding import PartitionSpec as P

HEAD = 64


highest = lax.Precision.HIGHEST


def sent_to_all(array, axis):
    copies = jnp.broadcast_to(array, (lax.axis_size(axis), *array.shape))
    return lax.all_to_all(copies, axis, split_axis=0, concat_axis=0, tiled=True)


def all_in_one(array, axis):
    leaves = jax.tree.leaves(array)
    sequence = sorted(range(len(leaves)), key=lambda k: -leaves[k].size)
    width = (1, *leaves[sequence[0]].shape)[-1]
    lines = [
        jnp.pad(leaves[k].reshape(-1), (0, -leaves[k].size % width)).reshape(-1, width)
        for k in sequence
    ]
    both, at, found = (sent_to_all(jnp.concatenate(lines), axis), 0, {})
    for k, line in zip(sequence, lines):
        piece = both[:, at : at + len(line)].reshape(len(both), -1)
        found[k] = piece[:, : leaves[k].size].reshape(-1, *leaves[k].shape)
        at += len(line)
    numbers = iter(range(len(leaves)))
    return jax.tree.map(lambda _: found[next(numbers)], array)


def combined_pairwise(pieces, combine):
    while len(jax.tree.leaves(pieces)[0]) > 1:
        pieces = jax.vmap(combine)(
            *(jax.tree.map(lambda part: part[side::2], pieces) for side in (0, 1))
        )
    return jax.tree.map(lambda part: part[0], pieces)


def entering(array, axis, combine, identity):
    length, mine = (lax.axis_size(axis), lax.axis_index(axis))
    passed = jnp.arange(length) > mine

    def kept(part, zero, own):
        part = jnp.where(
            passed.reshape(-1, *(1 for _ in own.shape)), part, jnp.asarray(zero, own.dtype)
        )
        return part[::-1]

    pieces = all_in_one(array, axis)
    return combined_pairwise(jax.tree.map(kept, pieces, identity, array), combine)


def in_blocks(array, dim, length):
    dims = array.shape
    tiles = array.reshape(*dims[:dim], length, dims[dim] // length, *dims[dim + 1 :])
    return jnp.moveaxis(tiles, dim, 0)


def sent_and_summed(array, axis, dim):
    length = lax.axis_size(axis)
    tiles = lax.all_to_all(in_blocks(array, dim, length), axis, 0, 0, tiled=True)
    return jnp.sum(tiles, axis=0)


def block_pass(state_in, pieces):
    grad_block, decay_block, step_block, b_block, c_block = pieces
    cum_decay = jnp.cumsum(decay_block, axis=1)
    gap_table = cum_decay[:, None, :] - cum_decay[:, :, None]
    upper_mask = lax.broadcasted_iota(jnp.int32, gap_table.shape, 2) >= lax.broadcasted_iota(
        jnp.int32, gap_table.shape, 1
    )
    weights = jnp.where(upper_mask, jnp.exp(jnp.where(upper_mask, gap_table, 0.0)), 0.0)
    intersection = lax.dot_general(
        b_block,
        c_block,
        (((0,), (0,)), ((), ())),
        precision=highest,
        preferred_element_type=jnp.float32,
    )
    within = jnp.einsum("hut,thp->uhp", weights * intersection[None], grad_block, precision=highest)
    tail_decay = jnp.exp(cum_decay[:, -1:] - cum_decay)
    from_state = (
        jnp.einsum("nu,hnp->uhp", b_block, state_in, precision=highest) * tail_decay.T[:, :, None]
    )
    result = step_block.T[:, :, None] * (within + from_state)
    state_out = jnp.einsum(
        "ht,nt,thp->hnp", jnp.exp(cum_decay), c_block, grad_block, precision=highest
    )
    state_out = state_out + jnp.exp(cum_decay[:, -1])[:, None, None] * state_in
    return (state_out, result)


def local_sweep(grad_rows, decay_rows, step_rows, b_rows, c_rows, start_state):
    row_count = grad_rows.shape[0]
    head_count = decay_rows.shape[0]
    block_len = min(512, row_count)
    block_count = row_count // block_len
    pieces = (
        grad_rows.reshape(block_count, block_len, head_count, grad_rows.shape[2]),
        decay_rows.reshape(head_count, block_count, block_len).transpose(1, 0, 2),
        step_rows.reshape(head_count, block_count, block_len).transpose(1, 0, 2),
        b_rows.reshape(b_rows.shape[0], block_count, block_len).transpose(1, 0, 2),
        c_rows.reshape(c_rows.shape[0], block_count, block_len).transpose(1, 0, 2),
    )
    state_out, results = lax.scan(block_pass, start_state, pieces, reverse=True)
    return (state_out, results.reshape(row_count, head_count, grad_rows.shape[2]))


def route_table(groups, expert, cap_len):
    hit_mask = jnp.any(groups == expert, axis=2)
    rank_ids = jnp.cumsum(hit_mask.astype(jnp.int32), axis=1) - 1
    slot_ids = lax.broadcasted_iota(jnp.int32, (1, 1, cap_len), 2)
    chosen = jnp.logical_and(hit_mask[:, :, None], rank_ids[:, :, None] == slot_ids)
    token_ids = lax.broadcasted_iota(jnp.int32, chosen.shape, 1)
    position = jnp.sum(jnp.where(chosen, token_ids, 0), axis=1)
    filled = jnp.any(chosen, axis=1)
    return (position, filled)


def slot_lookup(slot_table, own_ids, cap_len, expert_count):
    experts_iota = lax.broadcasted_iota(jnp.int32, (1, 1, expert_count), 2)
    onehot = own_ids[:, :, None] == experts_iota
    member = jnp.any(onehot, axis=1).astype(jnp.int32)
    rank_ids = jnp.cumsum(member, axis=0) - 1
    slot_of = jnp.sum(jnp.where(onehot, rank_ids[:, None, :], 0), axis=2)
    picked = jnp.sum(jnp.where(onehot[:, :, :, None], slot_table[None, None], 0.0), axis=2)
    slot_iota = lax.broadcasted_iota(jnp.int32, (1, 1, cap_len), 2)
    return jnp.sum(jnp.where(slot_of[:, :, None] == slot_iota, picked, 0.0), axis=2)


def shards(
    grad_out,
    out_proj,
    step_size,
    log_decay,
    b_input,
    c_output,
    skip_gain,
    expert_ids,
    hidden_act,
    w_down,
):
    exp_index = lax.axis_index("exp")
    exp_count = lax.axis_size("exp")
    seq_count = lax.axis_size("seq")
    tok_len = grad_out.shape[0]
    cap_len = hidden_act.shape[2]
    gathered = lax.all_gather(grad_out, "exp", axis=0, tiled=True)
    groups = expert_ids.reshape(exp_count, tok_len, expert_ids.shape[1])
    position, filled = route_table(groups, exp_index, cap_len)
    flat_index = (position + lax.broadcasted_iota(jnp.int32, position.shape, 0) * tok_len).reshape(
        -1
    )
    slot_rows = jnp.take(gathered, flat_index, axis=0)
    slot_rows = jnp.where(filled.reshape(-1, 1), slot_rows, jnp.zeros_like(slot_rows))
    saved_rows = hidden_act.reshape(-1, hidden_act.shape[3])
    weights = w_down[0]
    projected = lax.dot_general(
        lax.all_gather(slot_rows, "seq", axis=0, tiled=True),
        weights,
        (((1,), (1,)), ((), ())),
        preferred_element_type=jnp.float32,
    )
    partial_scores = jnp.sum(projected * saved_rows.astype(jnp.float32), axis=1)
    head_count = out_proj.shape[0] // HEAD
    inner_grad = lax.dot_general(
        gathered, out_proj, (((1,), (1,)), ((), ())), preferred_element_type=jnp.float32
    )
    row_count = inner_grad.shape[0]
    start_state = jnp.zeros((head_count, b_input.shape[0], HEAD), jnp.float32)
    summary, swept_part = local_sweep(
        inner_grad.reshape(row_count, head_count, HEAD),
        log_decay,
        step_size,
        b_input,
        c_output,
        start_state,
    )
    total_decay = jnp.sum(log_decay, axis=1)

    def combine(earlier, later_part):
        return (
            later_part[0] + jnp.exp(later_part[1])[:, None, None] * earlier[0],
            later_part[1] + earlier[1],
        )

    incoming, unused = entering(
        (summary, total_decay),
        "seq",
        combine,
        (jnp.zeros_like(summary), jnp.zeros_like(total_decay)),
    )
    suffix = jnp.flip(jnp.cumsum(jnp.flip(log_decay, 1), axis=1), 1) - log_decay
    from_carry = (
        jnp.einsum("nu,hnp->uhp", b_input, incoming, precision=highest)
        * jnp.exp(suffix).T[:, :, None]
    )
    combined = swept_part + step_size.T[:, :, None] * from_carry
    d_inner = (combined.reshape(row_count, -1) + skip_gain * inner_grad).astype(jnp.bfloat16)
    summed = sent_and_summed(partial_scores.reshape(seq_count, exp_count, cap_len), "seq", 0)
    slot_table = lax.all_to_all(
        summed.reshape(exp_count, 1, cap_len), "exp", split_axis=0, concat_axis=1, tiled=True
    ).reshape(exp_count, cap_len)
    own_ids = lax.dynamic_slice_in_dim(expert_ids, exp_index * tok_len, tok_len, 0)
    d_gate = slot_lookup(slot_table, own_ids, cap_len, exp_count).T
    return (d_inner, d_gate)


def solution(mesh):
    in_specs = (
        P(("seq", "exp"), None),
        P("exp", None),
        P("exp", "seq"),
        P("exp", "seq"),
        P(None, "seq"),
        P(None, "seq"),
        P("exp"),
        P("seq", None),
        P("exp", None, None, "seq"),
        P("exp", "seq", None),
    )
    out_specs = (P("seq", "exp"), P(None, ("seq", "exp")))
    return jax.shard_map(shards, mesh=mesh, in_specs=in_specs, out_specs=out_specs, check_vma=False)
```

profile of v0, /device:TPU:8, one launch (start us, length us, event | category | flops | bytes accessed | tf_op | source)
XLA Modules:
  0.0 358.2 jit_solution(10214156737029125887)
XLA Ops:
  10.4 102.3 %all-gather.3.cloned.1.call-done = bf16[2048,2048]{1,0:T(8,128)(2,1)} async-done(((bf16[128,2048]{1,0:T(8,128)(2,1)}), bf16[2048,2048]{1,0:T(8,128)(2,1)}) %all-gather.3.cloned.1.call-update) | async-done | bytes 8388624 | tf_op jit(solution)/shard_map/all_gather | solution.py:151
  112.7 8.8 %gather_fusion = bf16[288,2048]{1,0:T(8,128)(2,1)S(1)} fusion(bf16[2048,2048]{1,0:T(8,128)(2,1)} %all-gather.3.cloned.1.call-done, s32[1024]{0:T(1024)S(1)} %pad_clamp_fusion), kind=kCustom, calls=%fused_computation | custom fusion | bytes 2360448 | tf_op jit(solution)/shard_map/jit(_take)/gather | solution.py:157
  132.0 8.2 %fusion.56 = f32[2048,256]{1,0:T(8,128)} fusion(bf16[2048,2048]{1,0:T(8,128)(2,1)} %all-gather.3.cloned.1.call-done, bf16[256,2048]{1,0:T(8,128)(2,1)} %param.13), kind=kOutput, calls=%fused_computation.105 | convolution fusion | flops 2147483648 | bytes 11534336 | tf_op jit(solution)/shard_map/dot_general | solution.py:169
  140.2 5.1 %reshape.255 = f32[4,512,4,64]{3,2,1,0:T(4,128)} reshape(f32[2048,256]{1,0:T(8,128)} %fusion.56) | data formatting | bytes 4194304 | tf_op jit(solution)/shard_map/reshape;reshape | solution.py:102
  145.3 4.8 %copy.99 = f32[4,512,4,64]{1,3,2,0:T(8,128)} copy(f32[4,512,4,64]{3,2,1,0:T(4,128)} %reshape.255) | data formatting | bytes 4194304
  151.7 107.3 %while.17 = (s32[]{:T(128)}, f32[4,16,64]{2,1,0:T(8,128)S(1)}, f32[4,512,4,64]{1,0,3,2:T(4,128)}, f32[4,16,512]{2,0,1:T(4,128)S(1)}, f32[4,4,512]{2,1,0:T(4,128)...) while((s32[]{:T(128)}, f32[4,16,64]{2,1,0:T(8,128)S(1)}, ...), condition=%wide.region_3.4_spmd.clone, body=%wide.region_0.3_spmd.clone.sunk | while | flops 911919168 | bytes 7357060 | solution.py:108
  155.8 6.8 %fusion.80 = f32[512,4,64]{0,2,1:T(8,128)} fusion(f32[512,512]{1,0:T(8,128)S(1)} %fusion.79, f32[4,512]{1,0:T(4,128)S(1)} %bitcast.142, f32[4,512,4,64]{1,3,2,0:T(8,128)} %get-tuple-element.366, s32[]{:T(128)S(6)} %sub.117), kind=kOutput, calls=%fused_computation.16.clone.1 | convolution fusion | flops 810549248 | bytes 2113540 | tf_op jit(solution)/shard_map/while/body/eval_jaxpr/hut,thp->uhp/dot_general | solution.py:83
  167.4 11.2 %dynamic_update_slice.12 = f32[4,512,4,64]{1,0,3,2:T(4,128)} dynamic-update-slice(f32[4,512,4,64]{1,0,3,2:T(4,128)} %get-tuple-element.351, f32[1,512,4,64]{1,0,3,2:T(1,128)S(1)} %copy.176, s32[]{:T(128)S(6)} %sub.117, s32[]{:T(128)} %constant.95.clone.1..sunk, s32[]{:T(128)} %constant.95.clone.1..sunk, s32[]{:T(128)} %constant.95.clone.1..sunk) | dynamic-update-slice | bytes 1048580 | tf_op jit(solution)/shard_map/while/body/jit(dynamic_update_index_in_dim)/dynamic_update_slice | solution.py:108
  182.7 6.8 %fusion.80 = f32[512,4,64]{0,2,1:T(8,128)} fusion(f32[512,512]{1,0:T(8,128)S(1)} %fusion.79, f32[4,512]{1,0:T(4,128)S(1)} %bitcast.142, f32[4,512,4,64]{1,3,2,0:T(8,128)} %get-tuple-element.366, s32[]{:T(128)S(6)} %sub.117), kind=kOutput, calls=%fused_computation.16.clone.1 | convolution fusion | flops 810549248 | bytes 2113540 | tf_op jit(solution)/shard_map/while/body/eval_jaxpr/hut,thp->uhp/dot_general | solution.py:83
  194.3 11.1 %dynamic_update_slice.12 = f32[4,512,4,64]{1,0,3,2:T(4,128)} dynamic-update-slice(f32[4,512,4,64]{1,0,3,2:T(4,128)} %get-tuple-element.351, f32[1,512,4,64]{1,0,3,2:T(1,128)S(1)} %copy.176, s32[]{:T(128)S(6)} %sub.117, s32[]{:T(128)} %constant.95.clone.1..sunk, s32[]{:T(128)} %constant.95.clone.1..sunk, s32[]{:T(128)} %constant.95.clone.1..sunk) | dynamic-update-slice | bytes 1048580 | tf_op jit(solution)/shard_map/while/body/jit(dynamic_update_index_in_dim)/dynamic_update_slice | solution.py:108
  209.5 6.8 %fusion.80 = f32[512,4,64]{0,2,1:T(8,128)} fusion(f32[512,512]{1,0:T(8,128)S(1)} %fusion.79, f32[4,512]{1,0:T(4,128)S(1)} %bitcast.142, f32[4,512,4,64]{1,3,2,0:T(8,128)} %get-tuple-element.366, s32[]{:T(128)S(6)} %sub.117), kind=kOutput, calls=%fused_computation.16.clone.1 | convolution fusion | flops 810549248 | bytes 2113540 | tf_op jit(solution)/shard_map/while/body/eval_jaxpr/hut,thp->uhp/dot_general | solution.py:83
  221.1 11.1 %dynamic_update_slice.12 = f32[4,512,4,64]{1,0,3,2:T(4,128)} dynamic-update-slice(f32[4,512,4,64]{1,0,3,2:T(4,128)} %get-tuple-element.351, f32[1,512,4,64]{1,0,3,2:T(1,128)S(1)} %copy.176, s32[]{:T(128)S(6)} %sub.117, s32[]{:T(128)} %constant.95.clone.1..sunk, s32[]{:T(128)} %constant.95.clone.1..sunk, s32[]{:T(128)} %constant.95.clone.1..sunk) | dynamic-update-slice | bytes 1048580 | tf_op jit(solution)/shard_map/while/body/jit(dynamic_update_index_in_dim)/dynamic_update_slice | solution.py:108
  236.3 6.8 %fusion.80 = f32[512,4,64]{0,2,1:T(8,128)} fusion(f32[512,512]{1,0:T(8,128)S(1)} %fusion.79, f32[4,512]{1,0:T(4,128)S(1)} %bitcast.142, f32[4,512,4,64]{1,3,2,0:T(8,128)} %get-tuple-element.366, s32[]{:T(128)S(6)} %sub.117), kind=kOutput, calls=%fused_computation.16.clone.1 | convolution fusion | flops 810549248 | bytes 2113540 | tf_op jit(solution)/shard_map/while/body/eval_jaxpr/hut,thp->uhp/dot_general | solution.py:83
  247.9 11.1 %dynamic_update_slice.12 = f32[4,512,4,64]{1,0,3,2:T(4,128)} dynamic-update-slice(f32[4,512,4,64]{1,0,3,2:T(4,128)} %get-tuple-element.351, f32[1,512,4,64]{1,0,3,2:T(1,128)S(1)} %copy.176, s32[]{:T(128)S(6)} %sub.117, s32[]{:T(128)} %constant.95.clone.1..sunk, s32[]{:T(128)} %constant.95.clone.1..sunk, s32[]{:T(128)} %constant.95.clone.1..sunk) | dynamic-update-slice | bytes 1048580 | tf_op jit(solution)/shard_map/while/body/jit(dynamic_update_index_in_dim)/dynamic_update_slice | solution.py:108
  260.8 6.4 %all-to-all-start = ((f32[16,65,64]{1,2,0:T(8,128)}), f32[16,65,64]{1,2,0:T(8,128)S(1)}, u32[]{:S(2)}, u32[]{:S(2)}) async-start(f32[16,65,64]{1,2,0:T(8,128)} %broadcast_in_dim.137), calls=%async_computation | async-start | bytes 1048576 | tf_op jit(solution)/shard_map/all_to_all | solution.py:14
  268.1 10.0 %copy.111 = f32[1,256,18,512]{3,2,1,0:T(8,128)} copy(bf16[1,256,18,512]{3,1,2,0:T(8,128)(2,1)} %param.20) | data formatting | bytes 14155776 | tf_op jit(solution)/shard_map/convert_element_type | solution.py:167
  278.0 11.7 %reshape.242 = f32[4608,512]{1,0:T(8,128)} reshape(f32[1,256,18,512]{3,2,1,0:T(8,128)} %copy.111) | data formatting | bytes 18874368 | tf_op jit(solution)/shard_map/convert_element_type | solution.py:167
  289.8 9.7 %copy.112 = f32[4608,512]{0,1:T(8,128)} copy(f32[4608,512]{1,0:T(8,128)} %reshape.242) | data formatting | bytes 18874368 | tf_op jit(solution)/shard_map/convert_element_type | solution.py:167
  299.5 3.7 %reshape.234 = f32[2048,4,64]{0,2,1:T(8,128)} reshape(f32[4,512,4,64]{1,0,3,2:T(4,128)} %get-tuple-element.163) | data formatting | bytes 4194304 | tf_op jit(solution)/shard_map/reshape | solution.py:109
  304.6 15.4 %multiply_reduce_fusion = f32[4608]{0:T(1024)S(1)} fusion(f32[4608,512]{0,1:T(8,128)} %copy.112, bf16[4608,2048]{1,0:T(8,128)(2,1)} %all-gather.5.cloned.1.call-done, bf16[1,512,2048]{2,1,0:T(8,128)(2,1)S(1)} %copy-done), kind=kOutput, calls=%fused_computation.50 | convolution fusion | flops 9668390912 | bytes 30427136 | tf_op jit(solution)/shard_map/dot_general | solution.py:161
  320.9 7.2 %all-to-all-start.1 = ((f32[16,1,288]{2,1,0:T(1,128)}), f32[16,1,288]{2,1,0:T(1,128)S(1)}, u32[]{:S(2)}, u32[]{:S(2)}) async-start(f32[16,1,288]{2,1,0:T(1,128)} %reshape.259), calls=%async_computation.1 | async-start | bytes 49152 | tf_op jit(solution)/shard_map/all_to_all | solution.py:64
  328.2 5.0 %fusion.39 = f32[2048,4,64]{0,2,1:T(8,128)} fusion(f32[2048,4,64]{0,2,1:T(8,128)} %reshape.234, f32[2048,4]{0,1:T(4,128)S(1)} %copy-done.4, f32[2048,4]{0,1:T(4,128)S(1)} %bitcast.146, f32[16,2048]{1,0:T(8,128)S(1)} %copy-done.1, f32[2,4,16,64]{3,2,1,0:T(8,128)S(1)} %multiply_add_fusion.2, f32[4]{0:T(128)S(1)} %exponential_bitcast_fusion.3), kind=kOutput, calls=%fused_computation.54 | convolution fusion | flops 102244352 | bytes 4423696 | tf_op jit(solution)/shard_map/nu,hnp->uhp/dot_general | solution.py:198
  338.1 5.3 %all-to-all-start.2 = ((f32[16,1,18]{2,1,0:T(1,128)}), f32[16,1,18]{2,1,0:T(1,128)S(1)}, u32[]{:S(2)}, u32[]{:S(2)}) async-start(f32[16,1,18]{2,1,0:T(1,128)} %bitcast.20), calls=%async_computation.2 | async-start | bytes 16384 | tf_op jit(solution)/shard_map/all_to_all | solution.py:204
  346.9 3.6 %all-to-all-done.2 = f32[16,1,18]{2,1,0:T(1,128)S(1)} async-done(((f32[16,1,18]{2,1,0:T(1,128)}), f32[16,1,18]{2,1,0:T(1,128)S(1)}, u32[]{:S(2)}, u32[]{:S(2)}) %all-to-all-start.2) | async-done | bytes 1184 | tf_op jit(solution)/shard_map/all_to_all | solution.py:204
  (175 shorter events, 64.3 us)
Async XLA Ops:
  7.2 297.5 %copy-start = (bf16[1,512,2048]{2,1,0:T(8,128)(2,1)S(1)}, bf16[1,512,2048]{2,1,0:T(8,128)(2,1)}, u32[]{:S(2)}) copy-start(bf16[1,512,2048]{2,1,0:T(8,128)(2,1)} %param.21) | copy-start | bytes 6291460
  7.2 105.5 %all-gather.3.cloned.1.call-start = ((), (), s32[]{:S(2)}) async-start(), calls=%async_computation.3 | async-start | bytes 8912896 | tf_op jit(solution)/shard_map/all_gather | solution.py:151
  7.9 296.7 %all-gather.5.cloned.1.call-start = ((), (), s32[]{:S(2)}) async-start(), calls=%async_computation.4 | async-start | bytes 20054016 | tf_op jit(solution)/shard_map/all_gather | solution.py:162
  121.5 1.3 copy-start.5
  121.5 2.4 copy-start.2
  130.5 0.6 copy-start.7
  260.8 42.5 %all-to-all-start = ((f32[16,65,64]{1,2,0:T(8,128)}), f32[16,65,64]{1,2,0:T(8,128)S(1)}, u32[]{:S(2)}, u32[]{:S(2)}) async-start(f32[16,65,64]{1,2,0:T(8,128)} %broadcast_in_dim.137), calls=%async_computation | async-start | bytes 1048576 | tf_op jit(solution)/shard_map/all_to_all | solution.py:14
  289.8 9.7 %copy-start.8 = (s32[128,2]{0,1:T(2,128)S(1)}, s32[128,2]{0,1:T(2,128)}, u32[]{:S(2)}) copy-start(s32[128,2]{0,1:T(2,128)} %copy-done.7) | copy-start | bytes 3076
  304.6 23.6 %copy-start.1 = (f32[16,2048]{1,0:T(8,128)S(1)}, f32[16,2048]{1,0:T(8,128)}, u32[]{:S(2)}) copy-start(f32[16,2048]{1,0:T(8,128)} %param.16) | copy-start | bytes 393220
  304.6 23.6 %copy-start.3 = (f32[4,4,512]{2,1,0:T(4,128)S(1)}, f32[4,4,512]{2,1,0:T(4,128)}, u32[]{:S(2)}) copy-start(f32[4,4,512]{2,1,0:T(4,128)} %get-tuple-element.381) | copy-start | bytes 98308
  304.6 23.6 %copy-start.4 = (f32[2048,4]{0,1:T(4,128)S(1)}, f32[2048,4]{0,1:T(4,128)}, u32[]{:S(2)}) copy-start(f32[2048,4]{0,1:T(4,128)} %get-tuple-element.271) | copy-start | bytes 98308
  320.9 15.2 %all-to-all-start.1 = ((f32[16,1,288]{2,1,0:T(1,128)}), f32[16,1,288]{2,1,0:T(1,128)S(1)}, u32[]{:S(2)}, u32[]{:S(2)}) async-start(f32[16,1,288]{2,1,0:T(1,128)} %reshape.259), calls=%async_computation.1 | async-start | bytes 49152 | tf_op jit(solution)/shard_map/all_to_all | solution.py:64
  333.2 10.2 %copy-start.9 = (f32[256]{0:T(256)S(1)}, f32[256]{0:T(256)}, u32[]{:S(2)}) copy-start(f32[256]{0:T(256)} %param.18) | copy-start | bytes 3076
  338.1 12.4 %all-to-all-start.2 = ((f32[16,1,18]{2,1,0:T(1,128)}), f32[16,1,18]{2,1,0:T(1,128)S(1)}, u32[]{:S(2)}, u32[]{:S(2)}) async-start(f32[16,1,18]{2,1,0:T(1,128)} %bitcast.20), calls=%async_computation.2 | async-start | bytes 16384 | tf_op jit(solution)/shard_map/all_to_all | solution.py:204
  343.4 7.2 %copy-start.6 = (pred[128,2,16]{0,2,1:T(8,128)(4,1)S(1)}, pred[128,2,16]{0,2,1:T(8,128)(4,1)}, u32[]{:S(2)}) copy-start(pred[128,2,16]{0,2,1:T(8,128)(4,1)} %get-tuple-element.277) | copy-start | bytes 12292
Sparse Core Ops, SparseCore 0:
  9.8 102.8 all-gather.2
  122.9 122.2 all-gather.4
where the time goes:
time: 363 us; the launch traced here: 358 us
  local copies, waits for them, and re-layouts  119 us (33%)
  waiting for transfers between devices  107 us (29%)
  matrix products  73.1 us (20%)
  other arithmetic  25.6 us (7%)
  starting transfers between devices  19.1 us (5%)
  between operations  14.4 us (4%)
    all_gather x1, waiting for transfers between devices, shards(): gathered = lax.all_gather(grad_out, 'exp', axis=0, tiled=True)  102 us
    dynamic_update_slice x8, local copies, waits for them, and re-layouts, local_sweep(): state_out, results = lax.scan(block_pass, start_state, pieces, reverse=True)  46.8 us
    convert_element_type x3, local copies, waits for them, and re-layouts, shards(): partial_scores = jnp.sum(projected * saved_rows.astype(jnp.float32), axis=1)  31.3 us
    dot_general x4, matrix products, block_pass(): jnp.einsum('hut,thp->uhp', weights * intersection[None], grad_block, prec...  27.3 us
    dot_general x1, matrix products, shards(): lax.dot_general(lax.all_gather(slot_rows, 'seq', axis=0, tiled=True), wei...  15.4 us
    another operation x10, other arithmetic  9.24 us
    gather x1, local copies, waits for them, and re-layouts, shards(): slot_rows = jnp.take(gathered, flat_index, axis=0)  8.84 us
    dot_general x1, matrix products, shards(): lax.dot_general(gathered, out_proj, (((1,), (1,)), ((), ())), preferred_e...  8.21 us
  transfers between devices with their start and end apart: 5, of which 2 were waited for; matrix products, arithmetic and copies ran while one was open for 53% of the time, Pallas kernels for 0%

commit v1 on v0

v1 whole, which is shorter than its diff:
```python
import functools

import jax
import jax.numpy as jnp
from jax import lax
from jax.experimental import pallas as pl
from jax.experimental.pallas import tpu as pltpu
from jax.sharding import PartitionSpec as P

HEAD = 64
MESH = pl.DeviceIdType.MESH
F32, BF16 = jnp.float32, jnp.bfloat16

CAP = 18
HALF = (16, 32, 32, 32, 32)
OFF = (0, 16, 48, 80, 112)
BASE = (0, 256, 768, 1280, 1792)
RANK = (0, -1, 1, -2, 2, -3, 3, 4)
VMEM_ANY = pl.BlockSpec(memory_space=pltpu.VMEM)
HBM_ANY = pl.BlockSpec(memory_space=pl.ANY)


def dot_t(a, b):
    return lax.dot_general(a, b, (((1,), (1,)), ((), ())), preferred_element_type=F32)


def dot_n(a, b):
    return lax.dot_general(a, b, (((1,), (0,)), ((), ())), preferred_element_type=F32)


def dot_tn(a, b):
    return lax.dot_general(a, b, (((0,), (0,)), ((), ())), preferred_element_type=F32)


def halves(x):
    hi = x.astype(BF16)
    return hi, (x - hi.astype(F32)).astype(BF16)


def order_matrix(z, yl):
    row = lax.broadcasted_iota(jnp.int32, (288, 288), 0)
    col = lax.broadcasted_iota(jnp.int32, (288, 288), 1)
    late = row - 32
    side = jnp.where(row < 32, row >> 4, (late >> 5) & 1)
    place = jnp.where(row < 32, row & 15, 16 + ((late >> 6) << 5) + (late & 31))
    arrival = (place * 3641) >> 16
    slot = place - 18 * arrival
    shift = jnp.where((arrival & 1) == 1, -((arrival + 1) >> 1), arrival >> 1)
    source = (z + shift) & 7
    lane = jnp.where(side == 0, yl, 1 - yl)
    return col == slot * 16 + lane * 8 + source


def comm_kernel(
    g_hbm, w_hbm, ids, hid, wd_hbm, inner, scores,
    blocks, proj, outbox, rows, picks, wd, act, acts, keys, send, recv, local,
):
    s, e = lax.axis_index("seq"), lax.axis_index("exp")
    core, x, yh = s % 2, (s // 2) % 4, s // 8
    z, yl = e % 8, e // 8
    mine, other = yh * 4 + x, (1 - yh) * 4 + x
    plane = lambda yh_, x_: (yh_ * 4 + x_) * 2 + core
    zp, zm = (s, yl * 8 + (z + 1) % 8), (s, yl * 8 + (z + 7) % 8)
    xp, xm = (plane(yh, (x + 1) % 4), e), (plane(yh, (x + 3) % 4), e)
    yp, yq = (s, (1 - yl) * 8 + z), (plane(1 - yh, x), e)
    yd = (plane(1 - yh, x), (1 - yl) * 8 + z)
    sib = ((yh * 4 + x) * 2 + 1 - core, e)
    peers = (zp, zm, xp, xm, yp, yq, yd, sib)
    names, pending = {}, []

    def start(name, src, dst, to):
        i = names.setdefault(name, len(names))
        copy = pltpu.make_async_remote_copy(
            src_ref=src, dst_ref=dst, send_sem=send.at[i], recv_sem=recv.at[i],
            device_id=to, device_id_type=MESH,
        )
        copy.start()
        pending.append(copy)

    def arrived(name, dst):
        i = names[name]
        pltpu.make_async_remote_copy(
            src_ref=dst, dst_ref=dst, send_sem=send.at[i], recv_sem=recv.at[i],
            device_id=sib, device_id_type=MESH,
        ).wait_recv()

    def part(k, j, side=None):
        h = HALF[k]
        at = pl.multiple_of(BASE[k] + j * (2 * h), 2 * h)
        if side is None:
            return rows.at[pl.ds(at, 2 * h)]
        return rows.at[pl.ds(pl.multiple_of(at + side * h, 16), h)]

    spot = lambda a: (z + RANK[a] + 8) % 8
    loads = [
        pltpu.make_async_copy(g_hbm, blocks.at[z], local.at[0]),
        pltpu.make_async_copy(w_hbm, proj.at[yl], local.at[1]),
        pltpu.make_async_copy(wd_hbm, wd.at[core], local.at[2]),
        pltpu.make_async_copy(hid.at[:, :, core], act.at[core], local.at[3]),
    ]
    for load in loads:
        load.start()
    barrier = pltpu.get_barrier_semaphore()
    for peer in peers:
        pl.semaphore_signal(barrier, inc=1, device_id=peer, device_id_type=MESH)
    pl.semaphore_wait(barrier, len(peers))

    loads[0].wait()
    start("zp0", blocks.at[z], blocks.at[z], zp)
    start("zm0", blocks.at[z], blocks.at[z], zm)
    part_of_w = pl.ds(pl.multiple_of(core * 128, 128), 128)
    rest_of_w = pl.ds(pl.multiple_of((1 - core) * 128, 128), 128)
    loads[1].wait()
    start("w", proj.at[yl, part_of_w], proj.at[yl, part_of_w], yp)
    start("wd", wd_hbm, wd.at[core], sib)
    start("hid", hid.at[:, :, 1 - core], act.at[core], sib)

    for a in range(8):
        lanes = pl.ds(pl.multiple_of((yl * 8 + spot(a)) * 128, 128), 128)
        named = ids[:, lanes]
        for side, expert in ((0, e), (1, (1 - yl) * 8 + z)):
            hit = (named[0:1] == expert) | (named[1:2] == expert)
            keys[2 * a + side : 2 * a + side + 1, :] = jnp.where(hit, 1.0, 0.0)
    hits = keys[...]
    tri = lax.broadcasted_iota(jnp.int32, (128, 128), 0) <= lax.broadcasted_iota(
        jnp.int32, (128, 128), 1
    )
    rank = dot_n(hits.astype(BF16), jnp.where(tri, 1.0, 0.0).astype(BF16))
    keys[...] = jnp.where(hits > 0.5, rank - 1.0, -1000.0)

    def pick(k):
        h = HALF[k]
        place = lax.broadcasted_iota(jnp.int32, (h, 128), 0) + OFF[k]
        first, last = OFF[k] // CAP, (OFF[k] + h - 1) // CAP
        wanted = []
        for a in range(first, last + 1):
            at = (place - CAP * a).astype(F32)
            sides = [keys[2 * a + side : 2 * a + side + 1, :] == at for side in (0, 1)]
            wanted.append(
                jnp.concatenate([jnp.where(m, 1.0, 0.0) for m in sides], axis=0).astype(BF16)
            )
        for n in range(0, 2048, 512):
            found = None
            for a, chosen in zip(range(first, last + 1), wanted):
                more = dot_n(chosen, blocks[spot(a), :, n : n + 512])
                found = more if found is None else found + more
            found = found.astype(BF16)
            at = pl.multiple_of(BASE[k] + mine * (2 * h), 2 * h)
            rows[pl.ds(at, h), n : n + 512] = found[:h]
            picks[OFF[k] : OFF[k] + h, n : n + 512] = found[h:]

    def pick_and_send(k):
        pick(k)
        cut = picks.at[OFF[k] : OFF[k] + HALF[k]]
        start(f"pl{k}", cut, part(k, mine, 1), yp)
        start(f"pd{k}", cut, part(k, mine, 1), yd)
        start(f"ow{k}", part(k, mine, 0), part(k, mine, 0), yq)

    def spread(k):
        arrived(f"pl{k}", part(k, mine, 1))
        start(f"xpa{k}", part(k, mine), part(k, mine), xp)
        start(f"xma{k}", part(k, mine), part(k, mine), xm)
        arrived(f"pd{k}", part(k, other, 1))
        arrived(f"ow{k}", part(k, other, 0))
        start(f"xpb{k}", part(k, other), part(k, other), xp)
        start(f"xmb{k}", part(k, other), part(k, other), xm)

    def relay(k):
        for tag, side in (("a", yh), ("b", 1 - yh)):
            before, after = side * 4 + (x + 3) % 4, side * 4 + (x + 1) % 4
            arrived(f"xp{tag}{k}", part(k, before))
            start(f"fp{tag}{k}", part(k, before, 0), part(k, before, 0), xp)
            arrived(f"xm{tag}{k}", part(k, after))
            start(f"fm{tag}{k}", part(k, after, 1), part(k, after, 1), xm)

    def relayed(k):
        for tag, side in (("a", yh), ("b", 1 - yh)):
            far = side * 4 + (x + 2) % 4
            arrived(f"fp{tag}{k}", part(k, far, 0))
            arrived(f"fm{tag}{k}", part(k, far, 1))

    def ring(k):
        back, ahead = (z - k + 8) % 8, (z + k) % 8
        if k < 4:
            arrived(f"zp{k - 1}", blocks.at[back])
            arrived(f"zm{k - 1}", blocks.at[ahead])
        else:
            arrived("zp3", blocks.at[back, 0:64])
            arrived("zm3", blocks.at[ahead, 64:128])
        if k < 3:
            start(f"zp{k}", blocks.at[back], blocks.at[back], zp)
            start(f"zm{k}", blocks.at[ahead], blocks.at[ahead], zm)
        elif k == 3:
            start("zp3", blocks.at[back, 0:64], blocks.at[back, 0:64], zp)
            start("zm3", blocks.at[ahead, 64:128], blocks.at[ahead, 64:128], zm)

    def product(a):
        block = blocks[spot(a)]
        outbox[a] = dot_t(block, proj[1 - yl])
        to = pl.ds(pl.multiple_of((yl * 8 + spot(a)) * 128, 128), 128)
        start(f"c{a}", outbox.at[a], inner.at[to], yp)
        inner[to, :] = dot_t(block, proj[yl])

    def ordered():
        loads[3].wait()
        arrived("hid", act.at[1 - core])
        matrix = jnp.where(order_matrix(z, yl), 1.0, 0.0).astype(BF16)

        def step(i, _):
            j, c = i // 2, i % 2
            source = act[c, :, j].reshape(288, 512)
            put = dot_n(matrix, source).astype(BF16)
            for k in range(5):
                h = HALF[k]
                at = pl.multiple_of(BASE[k] + j * (2 * h), 2 * h)
                acts[c, pl.ds(at, 2 * h), :] = put[2 * OFF[k] : 2 * OFF[k] + 2 * h]
            return 0

        lax.fori_loop(0, 16, step, 0)

    def score(m):
        at = pl.multiple_of(m * 256, 256)
        lhs = rows[pl.ds(at, 256), :]

        def step(i, total):
            c, n = i // 2, pl.multiple_of((i % 2) * 256, 256)
            got = dot_t(lhs, wd[c, pl.ds(n, 256), :])
            prod = got * acts[c, pl.ds(at, 256), pl.ds(n, 256)].astype(F32)
            return total + prod[:, :128] + prod[:, 128:]

        total = lax.fori_loop(0, 4, step, jnp.zeros((256, 128), F32))
        scores[pl.ds(m, 1), :] = jnp.sum(total.T, axis=0, keepdims=True)

    pick_and_send(0)
    spread(0)
    ring(1)
    pick_and_send(1)
    arrived("w", proj.at[1 - yl, part_of_w])
    start("wf", proj.at[1 - yl, part_of_w], proj.at[1 - yl, part_of_w], sib)
    ordered()
    spread(1)
    ring(2)
    pick_and_send(2)
    arrived("wf", proj.at[1 - yl, rest_of_w])
    for a in range(3):
        product(a)
    spread(2)
    relay(0)
    ring(3)
    pick_and_send(3)
    for a in range(3, 5):
        product(a)
    spread(3)
    relay(1)
    ring(4)
    pick_and_send(4)
    for a in range(5, 8):
        product(a)
    spread(4)
    relay(2)
    for a in range(8):
        to = pl.ds(pl.multiple_of(((1 - yl) * 8 + spot(a)) * 128, 128), 128)
        arrived(f"c{a}", inner.at[to])
    loads[2].wait()
    arrived("wd", wd.at[1 - core])
    relayed(0)
    score(0)
    relay(3)
    relayed(1)
    lax.fori_loop(1, 3, lambda m, _: (score(m), 0)[1], 0)
    relay(4)
    for k in range(2, 5):
        relayed(k)
        lax.fori_loop(2 * k - 1, 2 * k + 1, lambda m, _: (score(m), 0)[1], 0)
    for copy in pending:
        copy.wait_send()


def chunk_decays(ld, cum, cum_t):
    lines = [
        jnp.concatenate([ld[:, 128 * i : 128 * (i + 1)], jnp.zeros((4, 128), F32)], axis=0)
        for i in range(16)
    ]
    x = jnp.concatenate(lines, axis=0)
    hi, rest = x.astype(BF16), None
    rest = x - hi.astype(F32)
    mid, low = halves(rest)
    tri = lax.broadcasted_iota(jnp.int32, (128, 128), 0) <= lax.broadcasted_iota(
        jnp.int32, (128, 128), 1
    )
    tri = jnp.where(tri, 1.0, 0.0).astype(BF16)
    total = (dot_n(low, tri) + dot_n(mid, tri)) + dot_n(hi, tri)
    for i in range(16):
        cum[i] = total[8 * i : 8 * i + 8]
    if cum_t is not None:
        turned = total.T
        for i in range(16):
            cum_t[i] = turned[:, 8 * i : 8 * i + 8]


def by_head(values):
    lane = lax.broadcasted_iota(jnp.int32, (1, 256), 1) // HEAD
    out = jnp.broadcast_to(values[3], (1, 256))
    for i in (2, 1, 0):
        out = jnp.where(lane == i, jnp.broadcast_to(values[i], (1, 256)), out)
    return out


def chunk_state(inner, c_in, cum, i):
    at = pl.ds(pl.multiple_of(i * 128, 128), 128)
    grown = jnp.exp(cum[i])
    c = c_in[:, at]
    hi, low = halves(jnp.concatenate([c * grown[h : h + 1] for h in range(4)], axis=0))
    g_hi, g_low = halves(inner[at, :])
    left = jnp.concatenate([hi, low, hi], axis=1)
    right = jnp.concatenate([g_hi, g_hi, g_low], axis=0)
    full = dot_n(left, right)
    lane = lax.broadcasted_iota(jnp.int32, (16, 256), 1) // HEAD
    out = full[48:64]
    for h in (2, 1, 0):
        out = jnp.where(lane == h, full[16 * h : 16 * h + 16], out)
    return out


def chunk_total(cum, i):
    ends = cum[i]
    return by_head([ends[h : h + 1, 127:128] for h in range(4)])


def summary_kernel(inner, ld, c_in, out, cum):
    chunk_decays(ld, cum, None)

    def step(n, carry):
        state, total = carry
        i = 15 - n
        ends = chunk_total(cum, i)
        return chunk_state(inner, c_in, cum, i) + jnp.exp(ends) * state, total + ends

    state, total = lax.fori_loop(
        0, 16, step, (jnp.zeros((16, 256), F32), jnp.zeros((1, 256), F32)), unroll=2
    )
    out[0:16] = state
    out[16:24] = jnp.broadcast_to(total, (8, 256))


def sweep_kernel(inner, ld, st, b_in, c_in, gain, states, out, cum, cum_t, step_t):
    me = lax.axis_index("seq")
    chunk_decays(ld, cum, cum_t)
    lines = [
        jnp.concatenate([st[:, 128 * i : 128 * (i + 1)], jnp.zeros((4, 128), F32)], axis=0)
        for i in range(16)
    ]
    turned = jnp.concatenate(lines, axis=0).T
    for i in range(16):
        step_t[i] = turned[:, 8 * i : 8 * i + 8]

    def enter(n, state):
        k = 15 - n
        got = states[k]
        return jnp.where(k > me, got[0:16] + jnp.exp(got[16:17]) * state, state)

    state = lax.fori_loop(0, 16, enter, jnp.zeros((16, 256), F32))
    upper = lax.broadcasted_iota(jnp.int32, (128, 128), 1) >= lax.broadcasted_iota(
        jnp.int32, (128, 128), 0
    )
    left_lanes = lax.broadcasted_iota(jnp.int32, (128, 128), 1) < HEAD
    gains = gain[...]

    def step(n, state):
        i = 15 - n
        at = pl.ds(pl.multiple_of(i * 128, 128), 128)
        b_hi, b_low = halves(b_in[:, at])
        c_hi, c_low = halves(c_in[:, at])
        b_all = jnp.concatenate([b_hi, b_low, b_hi], axis=0)
        table = dot_tn(b_all, jnp.concatenate([c_hi, c_hi, c_low], axis=0))
        s_hi, s_low = halves(state)
        carried = dot_tn(b_all, jnp.concatenate([s_hi, s_hi, s_low], axis=0))
        rows_, cols, steps = cum[i], cum_t[i], step_t[i]
        for p in (0, 1):
            lanes = slice(128 * p, 128 * p + 128)
            g = inner[at, lanes]
            tail, size = [], []
            m_hi, m_low = [], []
            for h in (2 * p, 2 * p + 1):
                col = jnp.broadcast_to(cols[:, h : h + 1], (128, 128))
                row = rows_[h : h + 1]
                gap = jnp.where(upper, row - col, 0.0)
                weight = jnp.where(upper, jnp.exp(gap), 0.0) * table
                hi, low = halves(weight)
                m_hi.append(hi)
                m_low.append(low)
                tail.append(jnp.exp(row[:, 127:128] - col))
                size.append(jnp.broadcast_to(steps[:, h : h + 1], (128, 128)))
            g_a, g_b = halves(jnp.where(left_lanes, g, 0.0)), halves(jnp.where(left_lanes, 0.0, g))
            left = jnp.concatenate(m_hi + m_low + m_hi, axis=1)
            right = jnp.concatenate([g_a[0], g_b[0], g_a[0], g_b[0], g_a[1], g_b[1]], axis=0)
            within = dot_n(left, right)
            tails = jnp.where(left_lanes, tail[0], tail[1])
            sizes = jnp.where(left_lanes, size[0], size[1])
            value = sizes * (within + carried[:, lanes] * tails) + gains[:, lanes] * g
            out[at, lanes] = value.astype(BF16)
        return chunk_state(inner, c_in, cum, i) + jnp.exp(chunk_total(cum, i)) * state

    lax.fori_loop(0, 16, step, state)


def slot_lookup(slot_table, own_ids, cap_len, expert_count):
    experts_iota = lax.broadcasted_iota(jnp.int32, (1, 1, expert_count), 2)
    onehot = own_ids[:, :, None] == experts_iota
    member = jnp.any(onehot, axis=1).astype(jnp.int32)
    rank_ids = jnp.cumsum(member, axis=0) - 1
    slot_of = jnp.sum(jnp.where(onehot, rank_ids[:, None, :], 0), axis=2)
    picked = jnp.sum(jnp.where(onehot[:, :, :, None], slot_table[None, None], 0.0), axis=2)
    slot_iota = lax.broadcasted_iota(jnp.int32, (1, 1, cap_len), 2)
    return jnp.sum(jnp.where(slot_of[:, :, None] == slot_iota, picked, 0.0), axis=2)


def shards(
    grad_out, out_proj, step_size, log_decay, b_input, c_output,
    skip_gain, expert_ids, hidden_act, w_down,
):
    s, e = lax.axis_index("seq"), lax.axis_index("exp")
    big = pltpu.CompilerParams(vmem_limit_bytes=60 * 1024 * 1024)
    hidden = hidden_act[0].transpose(1, 0, 2).reshape(18, 8, 2, 16, 512)
    inner, scores = pl.pallas_call(
        comm_kernel,
        name="gather_and_score",
        out_shape=(
            jax.ShapeDtypeStruct((2048, 256), F32),
            jax.ShapeDtypeStruct((9, 256), F32),
        ),
        in_specs=[HBM_ANY, HBM_ANY, VMEM_ANY, HBM_ANY, HBM_ANY],
        out_specs=(VMEM_ANY, VMEM_ANY),
        scratch_shapes=[
            pltpu.VMEM((8, 128, 2048), BF16),
            pltpu.VMEM((2, 256, 2048), BF16),
            pltpu.VMEM((8, 128, 256), F32),
            pltpu.VMEM((2304, 2048), BF16),
            pltpu.VMEM((144, 2048), BF16),
            pltpu.VMEM((2, 512, 2048), BF16),
            pltpu.VMEM((2, 18, 8, 16, 512), BF16),
            pltpu.VMEM((2, 2304, 512), BF16),
            pltpu.VMEM((16, 128), F32),
            pltpu.SemaphoreType.DMA((80,)),
            pltpu.SemaphoreType.DMA((80,)),
            pltpu.SemaphoreType.DMA((4,)),
        ],
        compiler_params=pltpu.CompilerParams(
            collective_id=0, has_side_effects=True, vmem_limit_bytes=60 * 1024 * 1024
        ),
    )(grad_out, out_proj, expert_ids.T, hidden, w_down[0])

    payload = pl.pallas_call(
        summary_kernel,
        name="summary",
        out_shape=jax.ShapeDtypeStruct((24, 256), F32),
        in_specs=[VMEM_ANY] * 3,
        out_specs=VMEM_ANY,
        scratch_shapes=[pltpu.VMEM((16, 8, 128), F32)],
        compiler_params=big,
    )(inner, log_decay, c_output)
    states = lax.all_to_all(
        jnp.broadcast_to(payload, (16, 24, 256)), "seq", split_axis=0, concat_axis=0, tiled=True
    )
    d_inner = pl.pallas_call(
        sweep_kernel,
        name="sweep",
        out_shape=jax.ShapeDtypeStruct((2048, 256), BF16),
        in_specs=[VMEM_ANY] * 7,
        out_specs=VMEM_ANY,
        scratch_shapes=[
            pltpu.VMEM((16, 8, 128), F32),
            pltpu.VMEM((16, 128, 8), F32),
            pltpu.VMEM((16, 128, 8), F32),
        ],
        compiler_params=big,
    )(inner, log_decay, step_size, b_input, c_output, skip_gain.reshape(1, 256), states)

    flat = scores.reshape(2304)
    late = flat[256:].reshape(4, 8, 64).transpose(1, 0, 2).reshape(8, 256)
    placed = jnp.concatenate([flat[:256].reshape(8, 32), late], axis=1)
    matrix = jnp.where(order_matrix(e % 8, e // 8), 1.0, 0.0)
    natural = jnp.dot(placed, matrix, precision=lax.Precision.HIGHEST)
    both = jnp.where((jnp.arange(2) == s % 2)[None, :, None], natural[:, None, :], 0.0)
    parts = lax.all_to_all(both.reshape(16, 288), "seq", 0, 0, tiled=True)
    summed = jnp.sum(parts, axis=0).reshape(18, 16).T
    slot_table = lax.all_to_all(
        summed.reshape(16, 1, 18), "exp", split_axis=0, concat_axis=1, tiled=True
    ).reshape(16, 18)
    own_ids = lax.dynamic_slice_in_dim(expert_ids, e * 128, 128, 0)
    d_gate = slot_lookup(slot_table, own_ids, 18, 16).T
    return d_inner, d_gate


def solution(mesh):
    in_specs = (
        P(("seq", "exp"), None),
        P("exp", None),
        P("exp", "seq"),
        P("exp", "seq"),
        P(None, "seq"),
        P(None, "seq"),
        P("exp"),
        P("seq", None),
        P("exp", None, None, "seq"),
        P("exp", "seq", None),
    )
    out_specs = (P("seq", "exp"), P(None, ("seq", "exp")))
    return jax.shard_map(shards, mesh=mesh, in_specs=in_specs, out_specs=out_specs, check_vma=False)
```

time: 363 us -> 169 us (0.47)
  Pallas kernels: 0 us -> 125 us
  local copies, waits for them, and re-layouts: 119 us -> 5.79 us
  waiting for transfers between devices: 107 us -> 19.4 us
  matrix products: 73.1 us -> 0.56 us
  other arithmetic: 25.6 us -> 1.71 us
  between operations: 14.4 us -> 0.75 us
  starting transfers between devices: 19.1 us -> 13.1 us
    pallas_call x0 -> x3, Pallas kernels: none -> 125 us  [the longest x1 110 us: shards(): pl.pallas_call(comm_kernel, name='gather_and_score', out_shape=(jax.Shape...]
    all_gather x2 -> x0, waiting for transfers between devices: 102 us -> none  [the longest x1 102 us: shards(): gathered = lax.all_gather(grad_out, 'exp', axis=0, tiled=True)]
    dot_general x19 -> x1, matrix products: 73.1 us -> 0.56 us  [shards(): natural = jnp.dot(placed, matrix, precision=lax.Precision.HIGHEST)]
    dynamic_update_slice x8 -> x0, local copies, waits for them, and re-layouts: 46.8 us -> none  [local_sweep(): state_out, results = lax.scan(block_pass, start_state, pieces, reverse=True)]
    convert_element_type x3 -> x0, local copies, waits for them, and re-layouts: 31.3 us -> none  [shards(): partial_scores = jnp.sum(projected * saved_rows.astype(jnp.float32), axis=1)]
    all_to_all x3, waiting for transfers between devices: 3.62 us -> 19.4 us  [the longest x1 9.71 us: shards(): lax.all_to_all(jnp.broadcast_to(payload, (16, 24, 256)), 'seq', split_axi...]
    another operation x11 -> x0, other arithmetic: 9.53 us -> none
    gather x1 -> x0, local copies, waits for them, and re-layouts: 8.84 us -> none  [shards(): slot_rows = jnp.take(gathered, flat_index, axis=0)]
  transfers between devices with their start and end apart: 5 -> 3, of which waited for: 2 -> 3; matrix products, arithmetic and copies ran while one was open for 53% -> 1% of each run, Pallas kernels for 0% -> 2%
where the time goes in v1:
time: 169 us; the launch traced here: 167 us
  Pallas kernels  125 us (74%)
  waiting for transfers between devices  19.4 us (11%)
  starting transfers between devices  13.1 us (8%)
  local copies, waits for them, and re-layouts  5.79 us (3%)
  other arithmetic  1.71 us (1%)
    pallas_call x1, Pallas kernels, shards(): pl.pallas_call(comm_kernel, name='gather_and_score', out_shape=(jax.Shape...  110 us
    pallas_call x1, Pallas kernels, shards(): pl.pallas_call(sweep_kernel, name='sweep', out_shape=jax.ShapeDtypeStruct...  11.5 us
    all_to_all x1, waiting for transfers between devices, shards(): lax.all_to_all(jnp.broadcast_to(payload, (16, 24, 256)), 'seq', split_axi...  9.71 us
    all_to_all x1, waiting for transfers between devices, shards(): parts = lax.all_to_all(both.reshape(16, 288), 'seq', 0, 0, tiled=True)  6.91 us
    all_to_all x1, starting transfers between devices, shards(): lax.all_to_all(summed.reshape(16, 1, 18), 'exp', split_axis=0, concat_axi...  5.99 us
    pallas_call x1, Pallas kernels, shards(): pl.pallas_call(summary_kernel, name='summary', out_shape=jax.ShapeDtypeSt...  3.97 us
    all_to_all x1, starting transfers between devices, shards(): lax.all_to_all(jnp.broadcast_to(payload, (16, 24, 256)), 'seq', split_axi...  3.55 us
    all_to_all x1, starting transfers between devices, shards(): parts = lax.all_to_all(both.reshape(16, 288), 'seq', 0, 0, tiled=True)  3.52 us
  transfers between devices with their start and end apart: 3, of which 3 were waited for; matrix products, arithmetic and copies ran while one was open for 1% of the time, Pallas kernels for 2%

profile of v1, /device:TPU:8, one launch (start us, length us, event | category | flops | bytes accessed | tf_op | source)
XLA Modules:
  0.0 166.7 jit_solution(16574876016703466986)
XLA Ops:
  0.7 109.9 %gather_and_score.1 = (f32[2048,256]{1,0:T(8,128)}, f32[9,256]{1,0:T(8,128)}) custom-call(bf16[128,2048]{1,0:T(8,128)(2,1)} %g_hbm.1, bf16[256,2048]{1,0:T(8,128)(2,1)} %w_hbm.1, s32[2,2048]{1,0:T(2,128)} %bitcast.21, bf16[18,8,2,16,512]{4,3,2,1,0:T(8,128)(2,1)} %bitcast.16, bf16[512,2048]{1,0:T(8,128)(2,1)} %bitcast.17), custom_call_target="tpu_custom_call" | custom-call | tf_op jit(solution)/shard_map/gather_and_score/pallas_call | solution.py:425
  110.5 0.7 slice_reduce_fusion
  111.3 0.7 slice.9
  112.0 0.1 broadcast_in_dim.94
  112.2 0.1 reshape.101
  112.3 0.6 fusion.15
  113.0 0.7 broadcast_select_fusion
  113.7 3.5 %all-to-all-start.1 = ((f32[16,1,288]{2,1,0:T(1,128)}), f32[16,1,288]{2,1,0:T(1,128)S(1)}, u32[]{:S(2)}, u32[]{:S(2)}) async-start(f32[16,1,288]{2,1,0:T(1,128)} %broadcast_select_fusion), calls=%async_computation.1 | async-start | bytes 49152 | tf_op jit(solution)/shard_map/all_to_all | solution.py:485
  117.2 0.7 constant_dynamic-slice_fusion
  117.9 6.9 %all-to-all-done.1 = f32[16,1,288]{2,1,0:T(1,128)S(1)} async-done(((f32[16,1,288]{2,1,0:T(1,128)}), f32[16,1,288]{2,1,0:T(1,128)S(1)}, u32[]{:S(2)}, u32[]{:S(2)}) %all-to-all-start.1) | async-done | bytes 18464 | tf_op jit(solution)/shard_map/all_to_all | solution.py:485
  124.9 0.7 copy.29
  125.6 6.0 %all-to-all-start.2 = ((f32[16,1,18]{2,1,0:T(1,128)}), f32[16,1,18]{2,1,0:T(1,128)S(1)}, u32[]{:S(2)}, u32[]{:S(2)}) async-start(f32[16,1,18]{2,1,0:T(1,128)} %copy.29), calls=%async_computation.2 | async-start | bytes 16384 | tf_op jit(solution)/shard_map/all_to_all | solution.py:487
  131.6 0.1 copy.25
  131.7 0.2 reduce_window_sum.11
  131.9 4.0 %summary.1 = f32[24,256]{1,0:T(8,128)} custom-call(f32[2048,256]{1,0:T(8,128)} %get-tuple-element.4.inner, f32[4,2048]{1,0:T(4,128)} %ld.3, f32[16,2048]{1,0:T(8,128)} %c_in.3), custom_call_target="tpu_custom_call" | custom-call | tf_op jit(solution)/shard_map/summary/pallas_call | solution.py:453
  135.8 2.8 %all-to-all-done.2 = f32[16,1,18]{2,1,0:T(1,128)S(1)} async-done(((f32[16,1,18]{2,1,0:T(1,128)}), f32[16,1,18]{2,1,0:T(1,128)S(1)}, u32[]{:S(2)}, u32[]{:S(2)}) %all-to-all-start.2) | async-done | bytes 1184 | tf_op jit(solution)/shard_map/all_to_all | solution.py:487
  138.6 1.5 broadcast_in_dim.89
  140.2 3.6 %all-to-all-start = ((f32[16,24,256]{2,1,0:T(8,128)}), f32[16,24,256]{2,1,0:T(8,128)S(1)}, u32[]{:S(2)}, u32[]{:S(2)}) async-start(f32[16,24,256]{2,1,0:T(8,128)} %broadcast_in_dim.89), calls=%async_computation | async-start | bytes 786432 | tf_op jit(solution)/shard_map/all_to_all | solution.py:462
  143.8 0.1 copy.30
  143.9 0.1 select_reduce_fusion
  144.1 0.6 select_reduce_fusion.1
  144.6 9.7 %all-to-all-done.states = f32[16,24,256]{2,1,0:T(8,128)S(1)} async-done(((f32[16,24,256]{2,1,0:T(8,128)}), f32[16,24,256]{2,1,0:T(8,128)S(1)}, u32[]{:S(2)}, u32[]{:S(2)}) %all-to-all-start) | async-done | bytes 393248 | tf_op jit(solution)/shard_map/all_to_all | solution.py:462
  154.4 0.8 copy-done
  155.1 11.5 %sweep.1 = bf16[2048,256]{1,0:T(8,128)(2,1)} custom-call(f32[2048,256]{1,0:T(8,128)} %get-tuple-element.4.inner, f32[4,2048]{1,0:T(4,128)} %ld.3, f32[4,2048]{1,0:T(4,128)} %st.1, f32[16,2048]{1,0:T(8,128)} %b_in.1, f32[16,2048]{1,0:T(8,128)} %c_in.3, f32[1,256]{1,0:T(1,128)} %bitcast.22, f32[16,24,256]{2,1,0:T(8,128)} %copy-done), custom_call_target="tpu_custom_call" | custom-call | tf_op jit(solution)/shard_map/sweep/pallas_call | solution.py:465
  (18 shorter events, 0.5 us)
Async XLA Ops:
  113.7 11.1 %all-to-all-start.1 = ((f32[16,1,288]{2,1,0:T(1,128)}), f32[16,1,288]{2,1,0:T(1,128)S(1)}, u32[]{:S(2)}, u32[]{:S(2)}) async-start(f32[16,1,288]{2,1,0:T(1,128)} %broadcast_select_fusion), calls=%async_computation.1 | async-start | bytes 49152 | tf_op jit(solution)/shard_map/all_to_all | solution.py:485
  125.6 13.1 %all-to-all-start.2 = ((f32[16,1,18]{2,1,0:T(1,128)}), f32[16,1,18]{2,1,0:T(1,128)S(1)}, u32[]{:S(2)}, u32[]{:S(2)}) async-start(f32[16,1,18]{2,1,0:T(1,128)} %copy.29), calls=%async_computation.2 | async-start | bytes 16384 | tf_op jit(solution)/shard_map/all_to_all | solution.py:487
  140.2 14.2 %all-to-all-start = ((f32[16,24,256]{2,1,0:T(8,128)}), f32[16,24,256]{2,1,0:T(8,128)S(1)}, u32[]{:S(2)}, u32[]{:S(2)}) async-start(f32[16,24,256]{2,1,0:T(8,128)} %broadcast_in_dim.89), calls=%async_computation | async-start | bytes 786432 | tf_op jit(solution)/shard_map/all_to_all | solution.py:462
  154.4 0.8 copy-start

commit v2 on v1

--- a/solution.py
+++ b/solution.py
@@ -1,5 +1,3 @@
-import functools
-
 import jax
 import jax.numpy as jnp
 from jax import lax
@@ -52,8 +50,9 @@
 
 
 def comm_kernel(
-    g_hbm, w_hbm, ids, hid, wd_hbm, inner, scores,
-    blocks, proj, outbox, rows, picks, wd, act, acts, keys, send, recv, local,
+    g_hbm, w_hbm, ids, hid, wd_hbm, ld, st, b_in, c_in, gain, out, gate,
+    inner, blocks, proj, outbox, rows, picks, wd, act, acts, keys, scores, sent, parts, tables,
+    cum, cum_t, step_t, pair, chips, send, recv, local,
 ):
     s, e = lax.axis_index("seq"), lax.axis_index("exp")
     core, x, yh = s % 2, (s // 2) % 4, s // 8
@@ -231,7 +230,97 @@
         total = lax.fori_loop(0, 4, step, jnp.zeros((256, 128), F32))
         scores[pl.ds(m, 1), :] = jnp.sum(total.T, axis=0, keepdims=True)
 
+    def score_chunk(k):
+        relayed(k)
+        if k == 0:
+            score(0)
+        else:
+            lax.fori_loop(2 * k - 1, 2 * k + 1, lambda m, _: (score(m), 0)[1], 0)
+        for j in range(8):
+            n = 2 * HALF[k]
+            m, at = (0, 32 * j) if k == 0 else (2 * k - 1 + j // 4, 64 * (j % 4))
+            sent[j, k : k + 1, 0:n] = scores[m : m + 1, at : at + n]
+
+    others = [(dy, dx) for dy in (0, 1) for dx in range(4) if dy or dx]
+    toward = lambda dy, dx: ((yh + dy) % 2, (x + dx) % 4)
+
+    def to_chips(tag, src_of, dst):
+        for dy, dx in others:
+            y_, x_ = toward(dy, dx)
+            start(f"{tag}{dy}{dx}", src_of(y_ * 4 + x_), dst.at[mine], (plane(y_, x_), e))
+
+    def from_chips(tag, dst):
+        for dy, dx in others:
+            y_, x_ = toward(dy, 4 - dx)
+            arrived(f"{tag}{dy}{dx}", dst.at[y_ * 4 + x_])
+
+    def summarize():
+        total = shard_summary(inner, c_in, cum)
+        pair[core] = total
+        start("pair", pair.at[core], pair.at[core], sib)
+
+    def combine_pair():
+        arrived("pair", pair.at[1 - core])
+        grown = jnp.exp(pair[0, 16:17])
+        chips[mine, 0:16] = pair[0, 0:16] + grown * pair[1, 0:16]
+        chips[mine, 16:24] = pair[0, 16:24] + pair[1, 16:24]
+        to_chips("st", lambda j: chips.at[mine], chips)
+
+    def entering():
+        from_chips("st", chips)
+
+        def enter(n, state):
+            k = 7 - n
+            got = chips[k]
+            return jnp.where(k > mine, got[0:16] + jnp.exp(got[16:17]) * state, state)
+
+        state = lax.fori_loop(0, 8, enter, jnp.zeros((16, 256), F32))
+        later = pair[1]
+        return jnp.where(core == 0, later[0:16] + jnp.exp(later[16:17]) * state, state)
+
+    def finish():
+        to_chips("sc", lambda j: sent.at[j], parts)
+        named = ids[:, pl.ds(pl.multiple_of(e * 128, 128), 128)]
+        expert = lax.broadcasted_iota(jnp.int32, (16, 128), 0)
+        hit = (named[0:1] == expert) | (named[1:2] == expert)
+        lower = lax.broadcasted_iota(jnp.int32, (128, 128), 0)
+        along = lax.broadcasted_iota(jnp.int32, (128, 128), 1)
+        upto = jnp.where(lower <= along, 1.0, 0.0).astype(BF16)
+        slot = dot_n(jnp.where(hit, 1.0, 0.0).astype(BF16), upto).astype(jnp.int32) - 1
+        off = (z - (expert & 7) + 8) & 7
+        place = 18 * jnp.where(off < 4, 2 * off, 15 - 2 * off) + slot
+        first = place < 16
+        chunk = jnp.where(first, 0, 1 + ((place - 16) >> 5))
+        spot_ = jnp.where(first, place, (place - 16) & 31)
+        lane = spot_ + jnp.where((expert >> 3) == yl, 0, jnp.where(first, 16, 32))
+        from_chips("sc", parts)
+        total = sent[mine]
+        for dy, dx in others:
+            y_, x_ = toward(dy, dx)
+            total = total + parts[y_ * 4 + x_]
+        tables[e] = total
+        for d in range(1, 16):
+            start(f"ex{d}", tables.at[e], tables.at[e], (s, (e + d) % 16))
+        for d in range(1, 16):
+            arrived(f"ex{d}", tables.at[(e + 16 - d) % 16])
+        row8 = lax.broadcasted_iota(jnp.int32, (8, 128), 0)
+        lines = [jnp.zeros((1, 128), F32), jnp.zeros((1, 128), F32)]
+        for i in range(16):
+            table = tables[i]
+            hi = table.astype(BF16)
+            mid, low = halves(table - hi.astype(F32))
+            chosen = jnp.where(lower == lane[i : i + 1], 1.0, 0.0).astype(BF16)
+            got = dot_n(jnp.concatenate([hi.astype(F32), mid.astype(F32), low.astype(F32)], axis=0).astype(BF16), chosen)
+            got = (got[16:24] + got[8:16]) + got[0:8]
+            got = jnp.sum(jnp.where(row8 == chunk[i : i + 1], got, 0.0), axis=0, keepdims=True)
+            for k in (0, 1):
+                lines[k] = jnp.where(named[k : k + 1] == i, got, lines[k])
+        gate[...] = jnp.concatenate(lines, axis=0)
+
+    sent[...] = jnp.zeros_like(sent)
     pick_and_send(0)
+    chunk_decays(ld, cum, cum_t)
+    turn_steps(st, step_t)
     spread(0)
     ring(1)
     pick_and_send(1)
@@ -261,17 +350,19 @@
     for a in range(8):
         to = pl.ds(pl.multiple_of(((1 - yl) * 8 + spot(a)) * 128, 128), 128)
         arrived(f"c{a}", inner.at[to])
+    summarize()
     loads[2].wait()
     arrived("wd", wd.at[1 - core])
-    relayed(0)
-    score(0)
+    score_chunk(0)
+    combine_pair()
+    score_chunk(1)
     relay(3)
-    relayed(1)
-    lax.fori_loop(1, 3, lambda m, _: (score(m), 0)[1], 0)
+    sweep(inner, b_in, c_in, gain, out, cum, cum_t, step_t, entering())
     relay(4)
-    for k in range(2, 5):
-        relayed(k)
-        lax.fori_loop(2 * k - 1, 2 * k + 1, lambda m, _: (score(m), 0)[1], 0)
+    score_chunk(2)
+    score_chunk(3)
+    score_chunk(4)
+    finish()
     for copy in pending:
         copy.wait_send()
 
@@ -327,9 +418,7 @@
     return by_head([ends[h : h + 1, 127:128] for h in range(4)])
 
 
-def summary_kernel(inner, ld, c_in, out, cum):
-    chunk_decays(ld, cum, None)
-
+def shard_summary(inner, c_in, cum):
     def step(n, carry):
         state, total = carry
         i = 15 - n
@@ -339,13 +428,10 @@
     state, total = lax.fori_loop(
         0, 16, step, (jnp.zeros((16, 256), F32), jnp.zeros((1, 256), F32)), unroll=2
     )
-    out[0:16] = state
-    out[16:24] = jnp.broadcast_to(total, (8, 256))
-
-
-def sweep_kernel(inner, ld, st, b_in, c_in, gain, states, out, cum, cum_t, step_t):
-    me = lax.axis_index("seq")
-    chunk_decays(ld, cum, cum_t)
+    return jnp.concatenate([state, jnp.broadcast_to(total, (8, 256))], axis=0)
+
+
+def turn_steps(st, step_t):
     lines = [
         jnp.concatenate([st[:, 128 * i : 128 * (i + 1)], jnp.zeros((4, 128), F32)], axis=0)
         for i in range(16)
@@ -354,12 +440,8 @@
     for i in range(16):
         step_t[i] = turned[:, 8 * i : 8 * i + 8]
 
-    def enter(n, state):
-        k = 15 - n
-        got = states[k]
-        return jnp.where(k > me, got[0:16] + jnp.exp(got[16:17]) * state, state)
-
-    state = lax.fori_loop(0, 16, enter, jnp.zeros((16, 256), F32))
+
+def sweep(inner, b_in, c_in, gain, out, cum, cum_t, step_t, state):
     upper = lax.broadcasted_iota(jnp.int32, (128, 128), 1) >= lax.broadcasted_iota(
         jnp.int32, (128, 128), 0
     )
@@ -404,34 +486,22 @@
     lax.fori_loop(0, 16, step, state)
 
 
-def slot_lookup(slot_table, own_ids, cap_len, expert_count):
-    experts_iota = lax.broadcasted_iota(jnp.int32, (1, 1, expert_count), 2)
-    onehot = own_ids[:, :, None] == experts_iota
-    member = jnp.any(onehot, axis=1).astype(jnp.int32)
-    rank_ids = jnp.cumsum(member, axis=0) - 1
-    slot_of = jnp.sum(jnp.where(onehot, rank_ids[:, None, :], 0), axis=2)
-    picked = jnp.sum(jnp.where(onehot[:, :, :, None], slot_table[None, None], 0.0), axis=2)
-    slot_iota = lax.broadcasted_iota(jnp.int32, (1, 1, cap_len), 2)
-    return jnp.sum(jnp.where(slot_of[:, :, None] == slot_iota, picked, 0.0), axis=2)
-
-
 def shards(
     grad_out, out_proj, step_size, log_decay, b_input, c_output,
     skip_gain, expert_ids, hidden_act, w_down,
 ):
-    s, e = lax.axis_index("seq"), lax.axis_index("exp")
-    big = pltpu.CompilerParams(vmem_limit_bytes=60 * 1024 * 1024)
     hidden = hidden_act[0].transpose(1, 0, 2).reshape(18, 8, 2, 16, 512)
-    inner, scores = pl.pallas_call(
+    return pl.pallas_call(
         comm_kernel,
-        name="gather_and_score",
+        name="mixer_and_router",
         out_shape=(
-            jax.ShapeDtypeStruct((2048, 256), F32),
-            jax.ShapeDtypeStruct((9, 256), F32),
+            jax.ShapeDtypeStruct((2048, 256), BF16),
+            jax.ShapeDtypeStruct((2, 128), F32),
         ),
-        in_specs=[HBM_ANY, HBM_ANY, VMEM_ANY, HBM_ANY, HBM_ANY],
+        in_specs=[HBM_ANY, HBM_ANY, VMEM_ANY, HBM_ANY, HBM_ANY] + [VMEM_ANY] * 5,
         out_specs=(VMEM_ANY, VMEM_ANY),
         scratch_shapes=[
+            pltpu.VMEM((2048, 256), F32),
             pltpu.VMEM((8, 128, 2048), BF16),
             pltpu.VMEM((2, 256, 2048), BF16),
             pltpu.VMEM((8, 128, 256), F32),
@@ -441,55 +511,26 @@
             pltpu.VMEM((2, 18, 8, 16, 512), BF16),
             pltpu.VMEM((2, 2304, 512), BF16),
             pltpu.VMEM((16, 128), F32),
-            pltpu.SemaphoreType.DMA((80,)),
-            pltpu.SemaphoreType.DMA((80,)),
+            pltpu.VMEM((9, 256), F32),
+            pltpu.VMEM((8, 8, 128), F32),
+            pltpu.VMEM((8, 8, 128), F32),
+            pltpu.VMEM((16, 8, 128), F32),
+            pltpu.VMEM((16, 8, 128), F32),
+            pltpu.VMEM((16, 128, 8), F32),
+            pltpu.VMEM((16, 128, 8), F32),
+            pltpu.VMEM((2, 24, 256), F32),
+            pltpu.VMEM((8, 24, 256), F32),
+            pltpu.SemaphoreType.DMA((112,)),
+            pltpu.SemaphoreType.DMA((112,)),
             pltpu.SemaphoreType.DMA((4,)),
         ],
         compiler_params=pltpu.CompilerParams(
             collective_id=0, has_side_effects=True, vmem_limit_bytes=60 * 1024 * 1024
         ),
-    )(grad_out, out_proj, expert_ids.T, hidden, w_down[0])
-
-    payload = pl.pallas_call(
-        summary_kernel,
-        name="summary",
-        out_shape=jax.ShapeDtypeStruct((24, 256), F32),
-        in_specs=[VMEM_ANY] * 3,
-        out_specs=VMEM_ANY,
-        scratch_shapes=[pltpu.VMEM((16, 8, 128), F32)],
-        compiler_params=big,
-    )(inner, log_decay, c_output)
-    states = lax.all_to_all(
-        jnp.broadcast_to(payload, (16, 24, 256)), "seq", split_axis=0, concat_axis=0, tiled=True
+    )(
+        grad_out, out_proj, expert_ids.T, hidden, w_down[0],
+        log_decay, step_size, b_input, c_output, skip_gain.reshape(1, 256),
     )
-    d_inner = pl.pallas_call(
-        sweep_kernel,
-        name="sweep",
-        out_shape=jax.ShapeDtypeStruct((2048, 256), BF16),
-        in_specs=[VMEM_ANY] * 7,
-        out_specs=VMEM_ANY,
-        scratch_shapes=[
-            pltpu.VMEM((16, 8, 128), F32),
-            pltpu.VMEM((16, 128, 8), F32),
-            pltpu.VMEM((16, 128, 8), F32),
-        ],
-        compiler_params=big,
-    )(inner, log_decay, step_size, b_input, c_output, skip_gain.reshape(1, 256), states)
-
-    flat = scores.reshape(2304)
-    late = flat[256:].reshape(4, 8, 64).transpose(1, 0, 2).reshape(8, 256)
-    placed = jnp.concatenate([flat[:256].reshape(8, 32), late], axis=1)
-    matrix = jnp.where(order_matrix(e % 8, e // 8), 1.0, 0.0)
-    natural = jnp.dot(placed, matrix, precision=lax.Precision.HIGHEST)
-    both = jnp.where((jnp.arange(2) == s % 2)[None, :, None], natural[:, None, :], 0.0)
-    parts = lax.all_to_all(both.reshape(16, 288), "seq", 0, 0, tiled=True)
-    summed = jnp.sum(parts, axis=0).reshape(18, 16).T
-    slot_table = lax.all_to_all(
-        summed.reshape(16, 1, 18), "exp", split_axis=0, concat_axis=1, tiled=True
-    ).reshape(16, 18)
-    own_ids = lax.dynamic_slice_in_dim(expert_ids, e * 128, 128, 0)
-    d_gate = slot_lookup(slot_table, own_ids, 18, 16).T
-    return d_inner, d_gate
 
 
 def solution(mesh):

time: 169 us -> 135 us (0.80); the launches traced: 167 us -> 135 us
  waiting for transfers between devices: 19.4 us -> 0 us
  starting transfers between devices: 13.1 us -> 0 us
  Pallas kernels: 125 us -> 130 us
  local copies, waits for them, and re-layouts: 5.79 us -> 3.5 us
  other arithmetic: 1.71 us -> 0 us
    all_to_all x3 -> x0, waiting for transfers between devices: 19.4 us -> none  [the longest x1 9.71 us: shards(): lax.all_to_all(jnp.broadcast_to(payload, (16, 24, 256)), 'seq', split_axi...]
    all_to_all x3 -> x0, starting transfers between devices: 13.1 us -> none  [the longest x1 5.99 us: shards(): lax.all_to_all(summed.reshape(16, 1, 18), 'exp', split_axis=0, concat_axi...]
    pallas_call x3 -> x1, Pallas kernels: 125 us -> 130 us  [shards(): pl.pallas_call(comm_kernel, name='mixer_and_router', out_shape=(jax.Shape...]
    unnamed x2, local copies, waits for them, and re-layouts: 0.76 us -> 3.5 us
    broadcast_in_dim x6 -> x0, local copies, waits for them, and re-layouts: 1.76 us -> none  [the longest x1 1.51 us: shards(): jnp.broadcast_to(payload, (16, 24, 256))]
  transfers between devices with their start and end apart: 3 -> 0, of which waited for: 3 -> 0; matrix products, arithmetic and copies ran while one was open for 1% -> 0% of each run, Pallas kernels for 2% -> 0%
where the time goes in v2:
time: 135 us
  Pallas kernels  130 us (96%)
  local copies, waits for them, and re-layouts  3.5 us (3%)
    pallas_call x1, Pallas kernels, shards(): pl.pallas_call(comm_kernel, name='mixer_and_router', out_shape=(jax.Shape...  130 us
    unnamed x2, local copies, waits for them, and re-layouts  3.5 us

profile of v2, /device:TPU:8, one launch (start us, length us, event | category | flops | bytes accessed | tf_op | source)
XLA Modules:
  0.0 134.6 jit_solution(16673250710131187459)
XLA Ops:
  0.6 130.4 %mixer_and_router.1 = (bf16[2048,256]{1,0:T(8,128)(2,1)}, f32[2,128]{1,0:T(2,128)}) custom-call(bf16[128,2048]{1,0:T(8,128)(2,1)} %g_hbm.1, bf16[256,2048]{1,0:T(8,128)(2,1)} %w_hbm.1, s32[2,2048]{1,0:T(2,128)} %bitcast.10, bf16[18,8,2,16,512]{4,3,2,1,0:T(8,128)(2,1)} %bitcast.8, bf16[512,2048]{1,0:T(8,128)(2,1)} %bitcast.9, f32[4,2048]{1,0:T(4,128)} %ld.1, ...), custom_call_target="tpu_custom_call" | custom-call | tf_op jit(solution)/shard_map/mixer_and_router/pallas_call | solution.py:494
  131.1 2.3 %copy.14 = bf16[2048,256]{1,0:T(8,128)(2,1)} copy(bf16[2048,256]{1,0:T(8,128)(2,1)} %get-tuple-element.4) | data formatting | bytes 2097152
  133.3 1.2 copy.15

commit v3 on v2

--- a/solution.py
+++ b/solution.py
@@ -10,9 +10,10 @@
 F32, BF16 = jnp.float32, jnp.bfloat16
 
 CAP = 18
-HALF = (16, 32, 32, 32, 32)
-OFF = (0, 16, 48, 80, 112)
-BASE = (0, 256, 768, 1280, 1792)
+HALF = (16, 32, 32, 32, 16, 16)
+OFF = (0, 16, 48, 80, 112, 128)
+BASE = (0, 256, 768, 1280, 1792, 2048)
+CHUNKS = len(HALF)
 RANK = (0, -1, 1, -2, 2, -3, 3, 4)
 VMEM_ANY = pl.BlockSpec(memory_space=pltpu.VMEM)
 HBM_ANY = pl.BlockSpec(memory_space=pl.ANY)
@@ -38,9 +39,12 @@
 def order_matrix(z, yl):
     row = lax.broadcasted_iota(jnp.int32, (288, 288), 0)
     col = lax.broadcasted_iota(jnp.int32, (288, 288), 1)
-    late = row - 32
-    side = jnp.where(row < 32, row >> 4, (late >> 5) & 1)
-    place = jnp.where(row < 32, row & 15, 16 + ((late >> 6) << 5) + (late & 31))
+    late, last = row - 32, row - 224
+    side = jnp.where(row < 32, row >> 4, jnp.where(row < 224, (late >> 5) & 1, (last >> 4) & 1))
+    middle = jnp.where(
+        row < 224, 16 + ((late >> 6) << 5) + (late & 31), 112 + ((last >> 5) << 4) + (last & 15)
+    )
+    place = jnp.where(row < 32, row & 15, middle)
     arrival = (place * 3641) >> 16
     slot = place - 18 * arrival
     shift = jnp.where((arrival & 1) == 1, -((arrival + 1) >> 1), arrival >> 1)
@@ -52,7 +56,7 @@
 def comm_kernel(
     g_hbm, w_hbm, ids, hid, wd_hbm, ld, st, b_in, c_in, gain, out, gate,
     inner, blocks, proj, outbox, rows, picks, wd, act, acts, keys, scores, sent, parts, tables,
-    cum, cum_t, step_t, pair, chips, send, recv, local,
+    cum, cum_t, step_t, states, pair, chips, send, recv, local,
 ):
     s, e = lax.axis_index("seq"), lax.axis_index("exp")
     core, x, yh = s % 2, (s // 2) % 4, s // 8
@@ -110,7 +114,6 @@
     part_of_w = pl.ds(pl.multiple_of(core * 128, 128), 128)
     rest_of_w = pl.ds(pl.multiple_of((1 - core) * 128, 128), 128)
     loads[1].wait()
-    start("w", proj.at[yl, part_of_w], proj.at[yl, part_of_w], yp)
     start("wd", wd_hbm, wd.at[core], sib)
     start("hid", hid.at[:, :, 1 - core], act.at[core], sib)
 
@@ -154,27 +157,34 @@
         start(f"pl{k}", cut, part(k, mine, 1), yp)
         start(f"pd{k}", cut, part(k, mine, 1), yd)
         start(f"ow{k}", part(k, mine, 0), part(k, mine, 0), yq)
+        to_both("a", k, mine, 0)
+
+    def to_both(tag, k, j, side):
+        start(f"xp{tag}{side}{k}", part(k, j, side), part(k, j, side), xp)
+        start(f"xm{tag}{side}{k}", part(k, j, side), part(k, j, side), xm)
 
     def spread(k):
         arrived(f"pl{k}", part(k, mine, 1))
-        start(f"xpa{k}", part(k, mine), part(k, mine), xp)
-        start(f"xma{k}", part(k, mine), part(k, mine), xm)
+        to_both("a", k, mine, 1)
         arrived(f"pd{k}", part(k, other, 1))
+        to_both("b", k, other, 1)
         arrived(f"ow{k}", part(k, other, 0))
-        start(f"xpb{k}", part(k, other), part(k, other), xp)
-        start(f"xmb{k}", part(k, other), part(k, other), xm)
+        to_both("b", k, other, 0)
 
     def relay(k):
         for tag, side in (("a", yh), ("b", 1 - yh)):
             before, after = side * 4 + (x + 3) % 4, side * 4 + (x + 1) % 4
-            arrived(f"xp{tag}{k}", part(k, before))
+            arrived(f"xp{tag}0{k}", part(k, before, 0))
             start(f"fp{tag}{k}", part(k, before, 0), part(k, before, 0), xp)
-            arrived(f"xm{tag}{k}", part(k, after))
+            arrived(f"xm{tag}1{k}", part(k, after, 1))
             start(f"fm{tag}{k}", part(k, after, 1), part(k, after, 1), xm)
 
     def relayed(k):
         for tag, side in (("a", yh), ("b", 1 - yh)):
+            before, after = side * 4 + (x + 3) % 4, side * 4 + (x + 1) % 4
             far = side * 4 + (x + 2) % 4
+            arrived(f"xp{tag}1{k}", part(k, before, 1))
+            arrived(f"xm{tag}0{k}", part(k, after, 0))
             arrived(f"fp{tag}{k}", part(k, far, 0))
             arrived(f"fm{tag}{k}", part(k, far, 1))
 
@@ -209,7 +219,7 @@
             j, c = i // 2, i % 2
             source = act[c, :, j].reshape(288, 512)
             put = dot_n(matrix, source).astype(BF16)
-            for k in range(5):
+            for k in range(CHUNKS):
                 h = HALF[k]
                 at = pl.multiple_of(BASE[k] + j * (2 * h), 2 * h)
                 acts[c, pl.ds(at, 2 * h), :] = put[2 * OFF[k] : 2 * OFF[k] + 2 * h]
@@ -232,14 +242,14 @@
 
     def score_chunk(k):
         relayed(k)
-        if k == 0:
-            score(0)
+        n, m = 2 * HALF[k], BASE[k] // 256
+        if n == 32:
+            score(m)
         else:
-            lax.fori_loop(2 * k - 1, 2 * k + 1, lambda m, _: (score(m), 0)[1], 0)
+            lax.fori_loop(m, m + 2, lambda i, _: (score(i), 0)[1], 0)
         for j in range(8):
-            n = 2 * HALF[k]
-            m, at = (0, 32 * j) if k == 0 else (2 * k - 1 + j // 4, 64 * (j % 4))
-            sent[j, k : k + 1, 0:n] = scores[m : m + 1, at : at + n]
+            at = n * j
+            sent[j, k : k + 1, 0:n] = scores[m + at // 256 : m + at // 256 + 1, at % 256 : at % 256 + n]
 
     others = [(dy, dx) for dy in (0, 1) for dx in range(4) if dy or dx]
     toward = lambda dy, dx: ((yh + dy) % 2, (x + dx) % 4)
@@ -254,8 +264,28 @@
             y_, x_ = toward(dy, 4 - dx)
             arrived(f"{tag}{dy}{dx}", dst.at[y_ * 4 + x_])
 
+    def chunk_of(a, side):
+        shift = (a // 2) * (1 - 2 * (a % 2)) - a % 2
+        return side * 8 + (z + shift + 8) % 8
+
+    def own_part(first, last):
+        for a in range(first, last):
+            product(a)
+        lax.fori_loop(first, last, lambda a, _: local_chunk(chunk_of(a, yl)), 0)
+
+    def other_part(first, last):
+        for a in range(first, last):
+            to = pl.ds(pl.multiple_of(((1 - yl) * 8 + spot(a)) * 128, 128), 128)
+            arrived(f"c{a}", inner.at[to])
+        lax.fori_loop(first, last, lambda a, _: local_chunk(chunk_of(a, 1 - yl)), 0)
+
+    def local_chunk(i):
+        states[i] = chunk_state(inner, c_in, cum, i)
+        within_chunk(inner, b_in, c_in, gain, cum, cum_t, step_t, i)
+        return 0
+
     def summarize():
-        total = shard_summary(inner, c_in, cum)
+        total = shard_summary(states, cum)
         pair[core] = total
         start("pair", pair.at[core], pair.at[core], sib)
 
@@ -280,6 +310,7 @@
 
     def finish():
         to_chips("sc", lambda j: sent.at[j], parts)
+        sweep(inner, b_in, out, cum, cum_t, step_t, states, entering())
         named = ids[:, pl.ds(pl.multiple_of(e * 128, 128), 128)]
         expert = lax.broadcasted_iota(jnp.int32, (16, 128), 0)
         hit = (named[0:1] == expert) | (named[1:2] == expert)
@@ -289,10 +320,10 @@
         slot = dot_n(jnp.where(hit, 1.0, 0.0).astype(BF16), upto).astype(jnp.int32) - 1
         off = (z - (expert & 7) + 8) & 7
         place = 18 * jnp.where(off < 4, 2 * off, 15 - 2 * off) + slot
-        first = place < 16
-        chunk = jnp.where(first, 0, 1 + ((place - 16) >> 5))
-        spot_ = jnp.where(first, place, (place - 16) & 31)
-        lane = spot_ + jnp.where((expert >> 3) == yl, 0, jnp.where(first, 16, 32))
+        wide = (place >= 16) & (place < 112)
+        chunk = jnp.where(wide, 1 + ((place - 16) >> 5), jnp.where(place < 16, 0, 4 + ((place - 112) >> 4)))
+        spot_ = jnp.where(wide, (place - 16) & 31, place & 15)
+        lane = spot_ + jnp.where((expert >> 3) == yl, 0, jnp.where(wide, 32, 16))
         from_chips("sc", parts)
         total = sent[mine]
         for dy, dx in others:
@@ -317,51 +348,58 @@
                 lines[k] = jnp.where(named[k : k + 1] == i, got, lines[k])
         gate[...] = jnp.concatenate(lines, axis=0)
 
+    def send_w(n):
+        at = pl.ds(pl.multiple_of(core * 128 + 64 * n, 64), 64)
+        start(f"w{n}", proj.at[yl, at], proj.at[yl, at], yd)
+
+    pick_and_send(0)
+    send_w(0)
     sent[...] = jnp.zeros_like(sent)
-    pick_and_send(0)
+    spread(0)
     chunk_decays(ld, cum, cum_t)
     turn_steps(st, step_t)
-    spread(0)
     ring(1)
     pick_and_send(1)
-    arrived("w", proj.at[1 - yl, part_of_w])
-    start("wf", proj.at[1 - yl, part_of_w], proj.at[1 - yl, part_of_w], sib)
+    send_w(1)
     ordered()
     spread(1)
     ring(2)
     pick_and_send(2)
+    for n in (0, 1):
+        arrived(f"w{n}", proj.at[1 - yl, pl.ds(pl.multiple_of(core * 128 + 64 * n, 64), 64)])
+    start("wf", proj.at[1 - yl, part_of_w], proj.at[1 - yl, part_of_w], sib)
+    relay(0)
+    spread(2)
     arrived("wf", proj.at[1 - yl, rest_of_w])
-    for a in range(3):
-        product(a)
-    spread(2)
-    relay(0)
+    own_part(0, 3)
     ring(3)
     pick_and_send(3)
-    for a in range(3, 5):
-        product(a)
+    relay(1)
     spread(3)
-    relay(1)
+    own_part(3, 5)
     ring(4)
     pick_and_send(4)
-    for a in range(5, 8):
-        product(a)
+    pick_and_send(5)
     spread(4)
+    spread(5)
+    own_part(5, 8)
+    other_part(0, 3)
     relay(2)
-    for a in range(8):
-        to = pl.ds(pl.multiple_of(((1 - yl) * 8 + spot(a)) * 128, 128), 128)
-        arrived(f"c{a}", inner.at[to])
-    summarize()
+    other_part(3, 5)
     loads[2].wait()
     arrived("wd", wd.at[1 - core])
     score_chunk(0)
-    combine_pair()
     score_chunk(1)
     relay(3)
-    sweep(inner, b_in, c_in, gain, out, cum, cum_t, step_t, entering())
+    other_part(5, 8)
+    summarize()
+    score_chunk(2)
+    combine_pair()
     relay(4)
-    score_chunk(2)
+    relay(5)
     score_chunk(3)
     score_chunk(4)
+    score_chunk(5)
     finish()
     for copy in pending:
         copy.wait_send()
@@ -418,15 +456,14 @@
     return by_head([ends[h : h + 1, 127:128] for h in range(4)])
 
 
-def shard_summary(inner, c_in, cum):
+def shard_summary(states, cum):
     def step(n, carry):
         state, total = carry
-        i = 15 - n
-        ends = chunk_total(cum, i)
-        return chunk_state(inner, c_in, cum, i) + jnp.exp(ends) * state, total + ends
+        ends = chunk_total(cum, 15 - n)
+        return states[15 - n] + jnp.exp(ends) * state, total + ends
 
     state, total = lax.fori_loop(
-        0, 16, step, (jnp.zeros((16, 256), F32), jnp.zeros((1, 256), F32)), unroll=2
+        0, 16, step, (jnp.zeros((16, 256), F32), jnp.zeros((1, 256), F32)), unroll=4
     )
     return jnp.concatenate([state, jnp.broadcast_to(total, (8, 256))], axis=0)
 
@@ -441,49 +478,63 @@
         step_t[i] = turned[:, 8 * i : 8 * i + 8]
 
 
-def sweep(inner, b_in, c_in, gain, out, cum, cum_t, step_t, state):
+def within_chunk(inner, b_in, c_in, gain, cum, cum_t, step_t, i):
     upper = lax.broadcasted_iota(jnp.int32, (128, 128), 1) >= lax.broadcasted_iota(
         jnp.int32, (128, 128), 0
     )
     left_lanes = lax.broadcasted_iota(jnp.int32, (128, 128), 1) < HEAD
     gains = gain[...]
+    at = pl.ds(pl.multiple_of(i * 128, 128), 128)
+    b_hi, b_low = halves(b_in[:, at])
+    c_hi, c_low = halves(c_in[:, at])
+    b_all = jnp.concatenate([b_hi, b_low, b_hi], axis=0)
+    table = dot_tn(b_all, jnp.concatenate([c_hi, c_hi, c_low], axis=0))
+    rows_, cols, steps = cum[i], cum_t[i], step_t[i]
+    for p in (0, 1):
+        lanes = slice(128 * p, 128 * p + 128)
+        g = inner[at, lanes]
+        size, m_hi, m_low = [], [], []
+        for h in (2 * p, 2 * p + 1):
+            col = jnp.broadcast_to(cols[:, h : h + 1], (128, 128))
+            gap = jnp.where(upper, rows_[h : h + 1] - col, 0.0)
+            weight = jnp.where(upper, jnp.exp(gap), 0.0) * table
+            hi, low = halves(weight)
+            m_hi.append(hi)
+            m_low.append(low)
+            size.append(jnp.broadcast_to(steps[:, h : h + 1], (128, 128)))
+        g_a, g_b = halves(jnp.where(left_lanes, g, 0.0)), halves(jnp.where(left_lanes, 0.0, g))
+        left = jnp.concatenate(m_hi + m_low + m_hi, axis=1)
+        right = jnp.concatenate([g_a[0], g_b[0], g_a[0], g_b[0], g_a[1], g_b[1]], axis=0)
+        sizes = jnp.where(left_lanes, size[0], size[1])
+        inner[at, lanes] = sizes * dot_n(left, right) + gains[:, lanes] * g
+
+
+def sweep(local, b_in, out, cum, cum_t, step_t, states, state):
+    left_lanes = lax.broadcasted_iota(jnp.int32, (128, 128), 1) < HEAD
 
     def step(n, state):
         i = 15 - n
         at = pl.ds(pl.multiple_of(i * 128, 128), 128)
         b_hi, b_low = halves(b_in[:, at])
-        c_hi, c_low = halves(c_in[:, at])
-        b_all = jnp.concatenate([b_hi, b_low, b_hi], axis=0)
-        table = dot_tn(b_all, jnp.concatenate([c_hi, c_hi, c_low], axis=0))
         s_hi, s_low = halves(state)
-        carried = dot_tn(b_all, jnp.concatenate([s_hi, s_hi, s_low], axis=0))
-        rows_, cols, steps = cum[i], cum_t[i], step_t[i]
+        carried = dot_tn(
+            jnp.concatenate([b_hi, b_low, b_hi], axis=0),
+            jnp.concatenate([s_hi, s_hi, s_low], axis=0),
+        )
+        ends, cols, steps = cum[i][:, 127:128], cum_t[i], step_t[i]
         for p in (0, 1):
             lanes = slice(128 * p, 128 * p + 128)
-            g = inner[at, lanes]
-            tail, size = [], []
-            m_hi, m_low = [], []
-            for h in (2 * p, 2 * p + 1):
-                col = jnp.broadcast_to(cols[:, h : h + 1], (128, 128))
-                row = rows_[h : h + 1]
-                gap = jnp.where(upper, row - col, 0.0)
-                weight = jnp.where(upper, jnp.exp(gap), 0.0) * table
-                hi, low = halves(weight)
-                m_hi.append(hi)
-                m_low.append(low)
-                tail.append(jnp.exp(row[:, 127:128] - col))
-                size.append(jnp.broadcast_to(steps[:, h : h + 1], (128, 128)))
-            g_a, g_b = halves(jnp.where(left_lanes, g, 0.0)), halves(jnp.where(left_lanes, 0.0, g))
-            left = jnp.concatenate(m_hi + m_low + m_hi, axis=1)
-            right = jnp.concatenate([g_a[0], g_b[0], g_a[0], g_b[0], g_a[1], g_b[1]], axis=0)
-            within = dot_n(left, right)
-            tails = jnp.where(left_lanes, tail[0], tail[1])
-            sizes = jnp.where(left_lanes, size[0], size[1])
-            value = sizes * (within + carried[:, lanes] * tails) + gains[:, lanes] * g
+            scale = [
+                jnp.broadcast_to(
+                    steps[:, h : h + 1] * jnp.exp(ends[h : h + 1] - cols[:, h : h + 1]), (128, 128)
+                )
+                for h in (2 * p, 2 * p + 1)
+            ]
+            value = local[at, lanes] + jnp.where(left_lanes, scale[0], scale[1]) * carried[:, lanes]
             out[at, lanes] = value.astype(BF16)
-        return chunk_state(inner, c_in, cum, i) + jnp.exp(chunk_total(cum, i)) * state
-
-    lax.fori_loop(0, 16, step, state)
+        return states[i] + jnp.exp(chunk_total(cum, i)) * state
+
+    lax.fori_loop(0, 16, step, state, unroll=2)
 
 
 def shards(
@@ -518,10 +569,11 @@
             pltpu.VMEM((16, 8, 128), F32),
             pltpu.VMEM((16, 128, 8), F32),
             pltpu.VMEM((16, 128, 8), F32),
+            pltpu.VMEM((16, 16, 256), F32),
             pltpu.VMEM((2, 24, 256), F32),
             pltpu.VMEM((8, 24, 256), F32),
-            pltpu.SemaphoreType.DMA((112,)),
-            pltpu.SemaphoreType.DMA((112,)),
+            pltpu.SemaphoreType.DMA((160,)),
+            pltpu.SemaphoreType.DMA((160,)),
             pltpu.SemaphoreType.DMA((4,)),
         ],
         compiler_params=pltpu.CompilerParams(

time: 135 us -> 125 us (0.926)
  Pallas kernels: 130 us -> 121 us
    pallas_call x1, Pallas kernels: 130 us -> 121 us  [shards(): pl.pallas_call(comm_kernel, name='mixer_and_router', out_shape=(jax.Shape...]
where the time goes in v3:
time: 125 us
  Pallas kernels  121 us (97%)
  local copies, waits for them, and re-layouts  3.5 us (3%)
    pallas_call x1, Pallas kernels, shards(): pl.pallas_call(comm_kernel, name='mixer_and_router', out_shape=(jax.Shape...  121 us
    unnamed x2, local copies, waits for them, and re-layouts  3.5 us

profile of v3, /device:TPU:8, one launch (start us, length us, event | category | flops | bytes accessed | tf_op | source)
XLA Modules:
  0.0 125.2 jit_solution(4450404173721682808)
XLA Ops:
  0.6 121.1 %mixer_and_router.1 = (bf16[2048,256]{1,0:T(8,128)(2,1)}, f32[2,128]{1,0:T(2,128)}) custom-call(bf16[128,2048]{1,0:T(8,128)(2,1)} %g_hbm.1, bf16[256,2048]{1,0:T(8,128)(2,1)} %w_hbm.1, s32[2,2048]{1,0:T(2,128)} %bitcast.10, bf16[18,8,2,16,512]{4,3,2,1,0:T(8,128)(2,1)} %bitcast.8, bf16[512,2048]{1,0:T(8,128)(2,1)} %bitcast.9, f32[4,2048]{1,0:T(4,128)} %ld.1, ...), custom_call_target="tpu_custom_call" | custom-call | tf_op jit(solution)/shard_map/mixer_and_router/pallas_call | solution.py:545
  121.7 2.3 %copy.14 = bf16[2048,256]{1,0:T(8,128)(2,1)} copy(bf16[2048,256]{1,0:T(8,128)(2,1)} %get-tuple-element.4) | data formatting | bytes 2097152
  124.0 1.2 copy.15

commit v4 on v3

--- a/solution.py
+++ b/solution.py
@@ -56,7 +56,7 @@
 def comm_kernel(
     g_hbm, w_hbm, ids, hid, wd_hbm, ld, st, b_in, c_in, gain, out, gate,
     inner, blocks, proj, outbox, rows, picks, wd, act, acts, keys, scores, sent, parts, tables,
-    cum, cum_t, step_t, states, pair, chips, send, recv, local,
+    cum, cum_t, step_t, states, pair, chips, chosen, send, recv, local,
 ):
     s, e = lax.axis_index("seq"), lax.axis_index("exp")
     core, x, yh = s % 2, (s // 2) % 4, s // 8
@@ -324,6 +324,13 @@
         chunk = jnp.where(wide, 1 + ((place - 16) >> 5), jnp.where(place < 16, 0, 4 + ((place - 112) >> 4)))
         spot_ = jnp.where(wide, (place - 16) & 31, place & 15)
         lane = spot_ + jnp.where((expert >> 3) == yl, 0, jnp.where(wide, 32, 16))
+        rows_of = []
+        for k in (0, 1):
+            for i in range(16):
+                both = (lower == lane[i : i + 1]) & (named[k : k + 1] == i)
+                chosen[k, 128 * i : 128 * i + 128, :] = jnp.where(both, 1.0, 0.0).astype(BF16)
+            own = jnp.where(expert == named[k : k + 1], chunk, 0)
+            rows_of.append(jnp.sum(own, axis=0, keepdims=True))
         from_chips("sc", parts)
         total = sent[mine]
         for dy, dx in others:
@@ -335,17 +342,15 @@
         for d in range(1, 16):
             arrived(f"ex{d}", tables.at[(e + 16 - d) % 16])
         row8 = lax.broadcasted_iota(jnp.int32, (8, 128), 0)
-        lines = [jnp.zeros((1, 128), F32), jnp.zeros((1, 128), F32)]
-        for i in range(16):
-            table = tables[i]
-            hi = table.astype(BF16)
-            mid, low = halves(table - hi.astype(F32))
-            chosen = jnp.where(lower == lane[i : i + 1], 1.0, 0.0).astype(BF16)
-            got = dot_n(jnp.concatenate([hi.astype(F32), mid.astype(F32), low.astype(F32)], axis=0).astype(BF16), chosen)
+        table = jnp.concatenate([tables[i] for i in range(16)], axis=1)
+        hi = table.astype(BF16)
+        mid, low = halves(table - hi.astype(F32))
+        thirds = jnp.concatenate([v.astype(F32) for v in (hi, mid, low)], axis=0).astype(BF16)
+        lines = []
+        for k in (0, 1):
+            got = dot_n(thirds, chosen[k])
             got = (got[16:24] + got[8:16]) + got[0:8]
-            got = jnp.sum(jnp.where(row8 == chunk[i : i + 1], got, 0.0), axis=0, keepdims=True)
-            for k in (0, 1):
-                lines[k] = jnp.where(named[k : k + 1] == i, got, lines[k])
+            lines.append(jnp.sum(jnp.where(row8 == rows_of[k], got, 0.0), axis=0, keepdims=True))
         gate[...] = jnp.concatenate(lines, axis=0)
 
     def send_w(n):
@@ -537,12 +542,17 @@
     lax.fori_loop(0, 16, step, state, unroll=2)
 
 
+def hand_over(d_in, gate_in, d_out, gate_out):
+    d_out[...] = d_in[...]
+    gate_out[...] = gate_in[...]
+
+
 def shards(
     grad_out, out_proj, step_size, log_decay, b_input, c_output,
     skip_gain, expert_ids, hidden_act, w_down,
 ):
     hidden = hidden_act[0].transpose(1, 0, 2).reshape(18, 8, 2, 16, 512)
-    return pl.pallas_call(
+    results = pl.pallas_call(
         comm_kernel,
         name="mixer_and_router",
         out_shape=(
@@ -572,6 +582,7 @@
             pltpu.VMEM((16, 16, 256), F32),
             pltpu.VMEM((2, 24, 256), F32),
             pltpu.VMEM((8, 24, 256), F32),
+            pltpu.VMEM((2, 2048, 128), BF16),
             pltpu.SemaphoreType.DMA((160,)),
             pltpu.SemaphoreType.DMA((160,)),
             pltpu.SemaphoreType.DMA((4,)),
@@ -583,6 +594,16 @@
         grad_out, out_proj, expert_ids.T, hidden, w_down[0],
         log_decay, step_size, b_input, c_output, skip_gain.reshape(1, 256),
     )
+    return pl.pallas_call(
+        hand_over,
+        name="hand_over",
+        out_shape=(
+            jax.ShapeDtypeStruct((2048, 256), BF16),
+            jax.ShapeDtypeStruct((2, 128), F32),
+        ),
+        in_specs=[VMEM_ANY] * 2,
+        out_specs=(VMEM_ANY, VMEM_ANY),
+    )(*results)
 
 
 def solution(mesh):

time: 125 us -> 124 us (level)
  local copies, waits for them, and re-layouts: 3.5 us -> 0 us
  Pallas kernels: 121 us -> 124 us
    unnamed x2 -> x0, local copies, waits for them, and re-layouts: 3.5 us -> none
    pallas_call x0 -> x1, Pallas kernels: none -> 2.27 us  [shards(): pl.pallas_call(hand_over, name='hand_over', out_shape=(jax.ShapeDtypeStru...]
where the time goes in v4:
time: 124 us
  Pallas kernels  124 us (100%)
    pallas_call x1, Pallas kernels, shards(): pl.pallas_call(comm_kernel, name='mixer_and_router', out_shape=(jax.Shape...  121 us

profile of v4, /device:TPU:8, one launch (start us, length us, event | category | flops | bytes accessed | tf_op | source)
XLA Modules:
  0.0 124.3 jit_solution(10715851931321345830)
XLA Ops:
  0.6 121.4 %mixer_and_router.1 = (bf16[2048,256]{1,0:T(8,128)(2,1)}, f32[2,128]{1,0:T(2,128)}) custom-call(bf16[128,2048]{1,0:T(8,128)(2,1)} %g_hbm.1, bf16[256,2048]{1,0:T(8,128)(2,1)} %w_hbm.1, s32[2,2048]{1,0:T(2,128)} %bitcast.10, bf16[18,8,2,16,512]{4,3,2,1,0:T(8,128)(2,1)} %bitcast.8, bf16[512,2048]{1,0:T(8,128)(2,1)} %bitcast.9, f32[4,2048]{1,0:T(4,128)} %ld.1, ...), custom_call_target="tpu_custom_call" | custom-call | tf_op jit(solution)/shard_map/mixer_and_router/pallas_call | solution.py:555
  122.0 2.3 %hand_over.1 = (bf16[2048,256]{1,0:T(8,128)(2,1)}, f32[2,128]{1,0:T(2,128)}) custom-call(bf16[2048,256]{1,0:T(8,128)(2,1)} %get-tuple-element.4.d_in, f32[2,128]{1,0:T(2,128)} %get-tuple-element.5.gate_in), custom_call_target="tpu_custom_call" | custom-call | tf_op jit(solution)/shard_map/hand_over/pallas_call | solution.py:597
